TPU v7x, 256 devices: a whole 4x4x8 slice. The times are simulated.
256 devices in a mesh: slab: 64 (over z, x, core), sub: 4 (over y).
Axes of the slice: x: 4, y: 4, z: 8, core: 2. Of those that a mesh axis runs over, the one named last changes fastest.
Arguments:
- values: float32 [6144, 2, 128, 256], P(('slab', 'sub')), may hold values from -0.25 to 0.25
- block_ids: int32 [6144, 2], P(('slab', 'sub')), may hold values from 0 to 3071, as said below
- tile_counts: int32 [64, 4], P('slab', 'sub'), may hold values from 8 to 24, as said below
- right_side: float32 [6144, 128], P(('slab', 'sub')), may hold values from -18 to 18
Outputs:
- solution: float32 [3072, 256], P(('slab', 'sub'))
- residual: float32 [6144, 128], P(('slab', 'sub'))
Inputs may be any that keep to these rules, and one draw needn't show every extreme that they name: `block_ids`: every block id names a node block held by a device of the row tile's own slab or of a slab one index of slab away; the first coupled block of each tile lies in its own slab. Block b is held by device b div 12. `tile_counts`: some device has all 24 slots live in every draw.
All inputs are finite; a program needn't handle non-finite values.
Results may differ from a plain program's by a relative error of at most 0.0003.
Values sent between devices are 32-bit elements; how exact they have to be, the bound alone decides.
A program may use at most 64 MiB of HBM per device.

v0:
```python
import functools

import jax
import jax.numpy as jnp
from jax import lax
from jax.sharding import Mesh
from jax.sharding import PartitionSpec as P

ITERS = 4
NB_DEV = 12
SLAB = ("slab_0", "slab_1", "slab_2")
SLAB_SUB = ("slab_0", "slab_1", "slab_2", "sub")


precise = lax.Precision.HIGHEST


def copy_for_each(value, axis):
    copies = jnp.broadcast_to(value, (lax.axis_size(axis), *value.shape))
    return lax.all_to_all(copies, axis, split_axis=0, concat_axis=0, tiled=True)


def in_order(parts, dim):
    lengths = list(parts.shape[1:])
    lengths[dim] *= parts.shape[0]
    return jnp.moveaxis(parts, 0, dim).reshape(lengths)


def gathered_copies(value, axis, dim):
    parts = copy_for_each(value, axis)
    return in_order(parts, dim)


def with_halo(block, sides, width):
    for axis, dim in sides:
        count = lax.axis_size(axis)
        forward = [(i, i + 1) for i in range(count - 1)]
        backward = [(target, source) for source, target in forward]
        low = lax.ppermute(
            lax.slice_in_dim(block, block.shape[dim] - width, None, axis=dim), axis, forward
        )
        high = lax.ppermute(lax.slice_in_dim(block, 0, width, axis=dim), axis, backward)
        block = jnp.concatenate([low, block, high], axis=dim)
    return block


def from_behind(block, axis, distance):
    devices = range(lax.axis_size(axis))
    route = [(i - distance, i) for i in devices if i - distance in devices]
    return lax.ppermute(block, axis, route)


def in_blocks(value, dim, count):
    before, after = (value.shape[:dim], value.shape[dim + 1 :])
    return jnp.moveaxis(value.reshape(*before, count, -1, *after), dim, 0)


def sent_and_summed(value, axis, dim):
    parts = in_blocks(value, dim, lax.axis_size(axis))
    arrived = lax.all_to_all(parts, axis, split_axis=0, concat_axis=0, tiled=True)
    return arrived.sum(axis=0)


def one_axis_at_a_time(value, axes):
    return functools.reduce(lax.psum, axes, value)


def per_device(values, block_ids, tile_counts, right_side):
    tiles_dev = values.shape[0]
    coupled = values.shape[1]
    block_len = values.shape[3]
    sub_count = lax.axis_size("sub")
    slab_index = lax.axis_index(SLAB)
    owner_dev = block_ids // NB_DEV
    rel_slab = owner_dev // sub_count - slab_index + 1
    window_ids = (rel_slab * sub_count + owner_dev % sub_count) * NB_DEV + block_ids % NB_DEV
    window_len = 3 * sub_count * NB_DEV
    selector = (
        window_ids.reshape(-1)[:, None] == jnp.arange(window_len, dtype=jnp.int32)[None, :]
    ).astype(jnp.float32)
    live_tiles = (jnp.arange(tiles_dev, dtype=jnp.int32) < tile_counts[0, 0]).astype(jnp.float32)

    def gather_window(field):
        gathered = gathered_copies(field, "sub", 0)
        return with_halo(gathered, ((SLAB, 0),), sub_count * NB_DEV)

    def return_window(contrib):
        pieces = contrib.reshape(3, sub_count * NB_DEV, block_len)
        from_above = from_behind(pieces[0], SLAB, -1)
        from_below = from_behind(pieces[2], SLAB, 1)
        return sent_and_summed(pieces[1] + from_above + from_below, "sub", 0)

    def forward(field):
        window = gather_window(field)
        picked = jnp.dot(selector, window, precision=precise).reshape(tiles_dev, coupled, block_len)
        image = jnp.einsum("tkij,tkj->ti", values, picked, precision=precise)
        return image * live_tiles[:, None]

    def spread_back(terms):
        flat_terms = terms.reshape(tiles_dev * coupled, block_len)
        return return_window(jnp.dot(selector.T, flat_terms, precision=precise))

    def backward(rows):
        return spread_back(jnp.einsum("tkij,ti->tkj", values, rows, precision=precise))

    squares = (
        jnp.einsum("tkij,tkij->tkj", values, values, precision=precise) * live_tiles[:, None, None]
    )
    jacobi = 1.0 / (1.0 + spread_back(squares))
    solution = jnp.zeros((NB_DEV, block_len), jnp.float32)
    residual = right_side * live_tiles[:, None]
    normal_res = backward(residual)
    scaled = jacobi * normal_res
    direction = scaled
    rho_now = one_axis_at_a_time(jnp.sum(normal_res * scaled), SLAB_SUB)
    for iteration in range(ITERS):
        image = forward(direction)
        back_image = backward(image)
        image_norm, cross_term, back_norm = (
            one_axis_at_a_time(jnp.sum(image * image), SLAB_SUB),
            one_axis_at_a_time(jnp.sum(scaled * back_image), SLAB_SUB),
            one_axis_at_a_time(jnp.sum(back_image * jacobi * back_image), SLAB_SUB),
        )
        step_size = rho_now / image_norm
        solution = solution + step_size * direction
        residual = residual - step_size * image
        normal_res = normal_res - step_size * back_image
        scaled = jacobi * normal_res
        rho_next = rho_now - 2.0 * step_size * cross_term + step_size * step_size * back_norm
        direction = scaled + rho_next / rho_now * direction
        rho_now = rho_next
    return (solution, residual)


def solution(mesh):
    split = Mesh(
        mesh.devices.reshape(8, 4, 2, mesh.shape["sub"]), ("slab_0", "slab_1", "slab_2", "sub")
    )
    placed = (P(SLAB_SUB, None, None, None), P(SLAB_SUB, None), P(SLAB, "sub"), P(SLAB_SUB, None))
    return jax.shard_map(
        per_device,
        mesh=split,
        in_specs=placed,
        out_specs=(P(SLAB_SUB, None), P(SLAB_SUB, None)),
        check_vma=False,
    )
```

profile of v0, /device:TPU:1, one launch (start us, length us, event | category | flops | bytes accessed | tf_op | source)
XLA Modules:
  0.0 388.6 jit_solution(1273834464946809145)
XLA Ops:
  1.3 0.8 broadcast_multiply_fusion.4
  2.1 5.1 %fusion.61 = f32[24,1,2,256]{3,1,2,0:T(1,128)S(1)} fusion(f32[24,128,1,1]{1,2,3,0:T(1,128)S(1)} %bitcast.74, f32[24,2,128,256]{3,2,1,0:T(8,128)} %param.4), kind=kOutput, calls=%fused_computation.103 | convolution fusion | flops 18874368 | bytes 6352896 | tf_op jit(solution)/shard_map/tkij,ti->tkj/dot_general | solution.py:104
  7.8 4.5 %collective-permute-start.1 = (f32[48,256]{1,0:T(8,128)S(1)}, f32[48,256]{1,0:T(8,128)S(1)}, u32[]{:S(2)}, u32[]{:S(2)}) collective-permute-start(f32[48,256]{1,0:T(8,128)S(1)} %get-tuple-element.68), channel_id=1, source_target_pairs={{0,4},{4,8},{8,12},{12,16},{16,20},{20,24},{24,28},{28,32},{32,36}... | collective-permute-start | bytes 147464 | tf_op jit(solution)/shard_map/ppermute | solution.py:50
  12.3 1.9 collective-permute-start
  14.3 3.6 multiply_reduce_fusion
  18.4 3.6 collective-permute-start.3
  22.0 1.9 collective-permute-start.2
  24.6 4.2 %all-to-all-start = ((f32[4,12,256]{2,1,0:T(8,128)}), f32[4,12,256]{2,1,0:T(8,128)S(1)}, u32[]{:S(2)}, u32[]{:S(2)}) async-start(f32[4,12,256]{2,1,0:T(8,128)} %reshape.105), calls=%async_computation | async-start | bytes 131072 | tf_op jit(solution)/shard_map/all_to_all | solution.py:60
  29.4 3.8 all-to-all-done
  33.3 3.3 all-to-all-start.1
  36.6 5.0 %all-to-all-done.1 = f32[4,12,256]{2,1,0:T(8,128)S(1)} async-done(((f32[4,12,256]{2,1,0:T(8,128)}), f32[4,12,256]{2,1,0:T(8,128)S(1)}, u32[]{:S(2)}, u32[]{:S(2)}) %all-to-all-start.1) | async-done | bytes 49184 | tf_op jit(solution)/shard_map/all_to_all | solution.py:60
  41.6 6.8 %all_to_all.45 = f32[4,12,256]{2,1,0:T(8,128)S(1)} all-to-all(f32[4,12,256]{2,1,0:T(8,128)S(1)} %broadcast_in_dim.8), channel_id=1, replica_groups=mesh['slab_0'=8,'slab_1'=4,'slab_2'=2,'sub'=4] {'sub'}, dimensions={0} | all-to-all | bytes 98304 | tf_op jit(solution)/shard_map/all_to_all | solution.py:20
  48.5 3.5 collective-permute-start.5
  52.0 5.2 %collective-permute-start.4 = (f32[48,256]{1,0:T(8,128)S(1)}, f32[48,256]{1,0:T(8,128)S(1)}, u32[]{:S(2)}, u32[]{:S(2)}) collective-permute-start(f32[48,256]{1,0:T(8,128)S(1)} %reshape.108), channel_id=1, source_target_pairs={{0,4},{4,8},{8,12},{12,16},{16,20},{20,24},{24,28},{28,32},{32,36}... | collective-permute-start | bytes 147464 | tf_op jit(solution)/shard_map/ppermute | solution.py:39
  57.2 1.1 collective-permute-done.4
  58.6 7.3 %fusion.62 = f32[24,1,128,1]{2,1,3,0:T(1,128)S(1)} fusion(f32[24,2,256,1]{2,3,1,0:T(1,128)S(1)} %reshape.141, f32[24,2,128,256]{3,2,1,0:T(8,128)} %param.4), kind=kOutput, calls=%fused_computation.104 | convolution fusion | flops 18874368 | bytes 6352896 | tf_op jit(solution)/shard_map/tkij,tkj->ti/dot_general | solution.py:96
  65.9 0.7 multiply_reduce_fusion.8
  66.6 5.1 %fusion.63 = f32[24,1,2,256]{3,1,2,0:T(1,128)S(1)} fusion(f32[24,128,1,1]{1,2,3,0:T(1,128)S(1)} %bitcast.66, f32[24,2,128,256]{3,2,1,0:T(8,128)} %param.4), kind=kOutput, calls=%fused_computation.105 | convolution fusion | flops 18874368 | bytes 6352896 | tf_op jit(solution)/shard_map/tkij,ti->tkj/dot_general | solution.py:104
  72.1 4.2 %collective-permute-start.7 = (f32[48,256]{1,0:T(8,128)S(1)}, f32[48,256]{1,0:T(8,128)S(1)}, u32[]{:S(2)}, u32[]{:S(2)}) collective-permute-start(f32[48,256]{1,0:T(8,128)S(1)} %get-tuple-element.64), channel_id=1, source_target_pairs={{0,4},{4,8},{8,12},{12,16},{16,20},{20,24},{24,28},{28,32},{32,36}... | collective-permute-start | bytes 147464 | tf_op jit(solution)/shard_map/ppermute | solution.py:50
  76.3 1.9 collective-permute-start.6
  78.3 3.5 collective-permute-done.6
  81.8 6.8 %all_to_all.46 = f32[4,12,256]{2,1,0:T(8,128)S(1)} all-to-all(f32[4,12,256]{2,1,0:T(8,128)S(1)} %reshape.111), channel_id=1, replica_groups=mesh['slab_0'=8,'slab_1'=4,'slab_2'=2,'sub'=4] {'sub'}, dimensions={0} | all-to-all | bytes 98304 | tf_op jit(solution)/shard_map/all_to_all | solution.py:60
  88.6 0.7 fusion.43
  89.3 20.3 %all-reduce.2 = (f32[]{:T(128)}, f32[]{:T(128)}, f32[]{:T(128)}, f32[]{:T(128)}) all-reduce(f32[]{:T(128)} %get-tuple-element.8, f32[]{:T(128)} %get-tuple-element.57, f32[]{:T(128)} %get-tuple-element.7, f32[]{:T(128)} %get-tuple-element.6), channel_id=1, replica_groups=mesh['slab_0'=8,'slab_1'=4,'slab_2'=2,'sub'=4] {'slab_0'}, use_global_device_ids=true, to_apply=%region_3.4 | all-reduce | flops 4 | bytes 32 | tf_op jit(solution)/shard_map/psum | solution.py:65
  109.6 17.7 %all-reduce.8 = (f32[]{:T(128)}, f32[]{:T(128)}, f32[]{:T(128)}, f32[]{:T(128)}) all-reduce(f32[]{:T(128)} %get-tuple-element.15, f32[]{:T(128)} %get-tuple-element.16, f32[]{:T(128)} %get-tuple-element.17, f32[]{:T(128)} %get-tuple-element.18), channel_id=1, replica_groups=mesh['slab_0'=8,'slab_1'=4,'slab_2'=2,'sub'=4] {'slab_1'}, use_global_device_ids=true, to_apply=%region_4.5 | all-reduce | flops 4 | bytes 32 | tf_op jit(solution)/shard_map/psum | solution.py:65
  127.3 4.1 %all-reduce.11 = (f32[]{:T(128)}, f32[]{:T(128)}, f32[]{:T(128)}, f32[]{:T(128)}) all-reduce(f32[]{:T(128)} %get-tuple-element.35, f32[]{:T(128)} %get-tuple-element.36, f32[]{:T(128)} %get-tuple-element.37, f32[]{:T(128)} %get-tuple-element.38), channel_id=1, replica_groups=mesh['slab_0'=8,'slab_1'=4,'slab_2'=2,'sub'=4] {'slab_2'}, use_global_device_ids=true, to_apply=%region_5.6 | all-reduce | flops 4 | bytes 32 | tf_op jit(solution)/shard_map/psum | solution.py:65
  131.4 7.6 %all-reduce.5 = (f32[]{:T(128)}, f32[]{:T(128)}, f32[]{:T(128)}, f32[]{:T(128)}) all-reduce(f32[]{:T(128)} %get-tuple-element.45, f32[]{:T(128)} %get-tuple-element.46, f32[]{:T(128)} %get-tuple-element.47, f32[]{:T(128)} %get-tuple-element.48), channel_id=1, replica_groups=mesh['slab_0'=8,'slab_1'=4,'slab_2'=2,'sub'=4] {'sub'}, use_global_device_ids=true, to_apply=%region_6.7 | all-reduce | flops 4 | bytes 32 | tf_op jit(solution)/shard_map/psum | solution.py:65
  142.9 6.8 %all_to_all.47 = f32[4,12,256]{2,1,0:T(8,128)S(1)} all-to-all(f32[4,12,256]{2,1,0:T(8,128)S(1)} %broadcast_in_dim.9), channel_id=1, replica_groups=mesh['slab_0'=8,'slab_1'=4,'slab_2'=2,'sub'=4] {'sub'}, dimensions={0} | all-to-all | bytes 98304 | tf_op jit(solution)/shard_map/all_to_all | solution.py:20
  149.8 5.4 %collective-permute-start.9 = (f32[48,256]{1,0:T(8,128)S(1)}, f32[48,256]{1,0:T(8,128)S(1)}, u32[]{:S(2)}, u32[]{:S(2)}) collective-permute-start(f32[48,256]{1,0:T(8,128)S(1)} %reshape.112), channel_id=1, source_target_pairs={{4,0},{8,4},{12,8},{16,12},{20,16},{24,20},{28,24},{32,28},{36,32}... | collective-permute-start | bytes 147464 | tf_op jit(solution)/shard_map/ppermute | solution.py:42
  155.2 3.7 collective-permute-start.8
  158.9 1.0 collective-permute-done.8
  160.2 7.3 %fusion.64 = f32[24,1,128,1]{2,1,3,0:T(1,128)S(1)} fusion(f32[24,2,256,1]{2,3,1,0:T(1,128)S(1)} %reshape.143, f32[24,2,128,256]{3,2,1,0:T(8,128)} %param.4), kind=kOutput, calls=%fused_computation.106 | convolution fusion | flops 18874368 | bytes 6352896 | tf_op jit(solution)/shard_map/tkij,tkj->ti/dot_general | solution.py:96
  168.1 5.1 %fusion.65 = f32[24,1,2,256]{3,1,2,0:T(1,128)S(1)} fusion(f32[24,128,1,1]{1,2,3,0:T(1,128)S(1)} %bitcast.67, f32[24,2,128,256]{3,2,1,0:T(8,128)} %param.4), kind=kOutput, calls=%fused_computation.107 | convolution fusion | flops 18874368 | bytes 6352896 | tf_op jit(solution)/shard_map/tkij,ti->tkj/dot_general | solution.py:104
  173.6 4.2 %collective-permute-start.11 = (f32[48,256]{1,0:T(8,128)S(1)}, f32[48,256]{1,0:T(8,128)S(1)}, u32[]{:S(2)}, u32[]{:S(2)}) collective-permute-start(f32[48,256]{1,0:T(8,128)S(1)} %get-tuple-element.62), channel_id=1, source_target_pairs={{0,4},{4,8},{8,12},{12,16},{16,20},{20,24},{24,28},{28,32},{32,36}... | collective-permute-start | bytes 147464 | tf_op jit(solution)/shard_map/ppermute | solution.py:50
  177.9 1.9 collective-permute-start.10
  179.8 3.5 collective-permute-done.10
  183.3 6.8 %all_to_all.48 = f32[4,12,256]{2,1,0:T(8,128)S(1)} all-to-all(f32[4,12,256]{2,1,0:T(8,128)S(1)} %reshape.115), channel_id=1, replica_groups=mesh['slab_0'=8,'slab_1'=4,'slab_2'=2,'sub'=4] {'sub'}, dimensions={0} | all-to-all | bytes 98304 | tf_op jit(solution)/shard_map/all_to_all | solution.py:60
  190.8 14.6 %all-reduce.1 = (f32[]{:T(128)}, f32[]{:T(128)}, f32[]{:T(128)}) all-reduce(f32[]{:T(128)} %get-tuple-element.53, f32[]{:T(128)} %get-tuple-element.5, f32[]{:T(128)} %get-tuple-element.4), channel_id=1, replica_groups=mesh['slab_0'=8,'slab_1'=4,'slab_2'=2,'sub'=4] {'slab_0'}, use_global_device_ids=true, to_apply=%region_24.25 | all-reduce | flops 3 | bytes 24 | tf_op jit(solution)/shard_map/psum | solution.py:65
  205.4 13.6 %all-reduce.7 = (f32[]{:T(128)}, f32[]{:T(128)}, f32[]{:T(128)}) all-reduce(f32[]{:T(128)} %get-tuple-element.12, f32[]{:T(128)} %get-tuple-element.13, f32[]{:T(128)} %get-tuple-element.14), channel_id=1, replica_groups=mesh['slab_0'=8,'slab_1'=4,'slab_2'=2,'sub'=4] {'slab_1'}, use_global_device_ids=true, to_apply=%region_25.26 | all-reduce | flops 3 | bytes 24 | tf_op jit(solution)/shard_map/psum | solution.py:65
  218.9 4.8 %all-reduce.10 = (f32[]{:T(128)}, f32[]{:T(128)}, f32[]{:T(128)}) all-reduce(f32[]{:T(128)} %get-tuple-element.32, f32[]{:T(128)} %get-tuple-element.33, f32[]{:T(128)} %get-tuple-element.34), channel_id=1, replica_groups=mesh['slab_0'=8,'slab_1'=4,'slab_2'=2,'sub'=4] {'slab_2'}, use_global_device_ids=true, to_apply=%region_26.27 | all-reduce | flops 3 | bytes 24 | tf_op jit(solution)/shard_map/psum | solution.py:65
  223.8 7.5 %all-reduce.4 = (f32[]{:T(128)}, f32[]{:T(128)}, f32[]{:T(128)}) all-reduce(f32[]{:T(128)} %get-tuple-element.42, f32[]{:T(128)} %get-tuple-element.43, f32[]{:T(128)} %get-tuple-element.44), channel_id=1, replica_groups=mesh['slab_0'=8,'slab_1'=4,'slab_2'=2,'sub'=4] {'sub'}, use_global_device_ids=true, to_apply=%region_27.28 | all-reduce | flops 3 | bytes 24 | tf_op jit(solution)/shard_map/psum | solution.py:65
  233.2 6.8 %all_to_all.49 = f32[4,12,256]{2,1,0:T(8,128)S(1)} all-to-all(f32[4,12,256]{2,1,0:T(8,128)S(1)} %broadcast_in_dim.10), channel_id=1, replica_groups=mesh['slab_0'=8,'slab_1'=4,'slab_2'=2,'sub'=4] {'sub'}, dimensions={0} | all-to-all | bytes 98304 | tf_op jit(solution)/shard_map/all_to_all | solution.py:20
  240.1 5.4 %collective-permute-start.13 = (f32[48,256]{1,0:T(8,128)S(1)}, f32[48,256]{1,0:T(8,128)S(1)}, u32[]{:S(2)}, u32[]{:S(2)}) collective-permute-start(f32[48,256]{1,0:T(8,128)S(1)} %reshape.116), channel_id=1, source_target_pairs={{4,0},{8,4},{12,8},{16,12},{20,16},{24,20},{28,24},{32,28},{36,32}... | collective-permute-start | bytes 147464 | tf_op jit(solution)/shard_map/ppermute | solution.py:42
  245.5 3.5 collective-permute-start.12
  249.0 1.1 collective-permute-done.12
  250.5 7.3 %fusion.66 = f32[24,1,128,1]{2,1,3,0:T(1,128)S(1)} fusion(f32[24,2,256,1]{2,3,1,0:T(1,128)S(1)} %reshape.145, f32[24,2,128,256]{3,2,1,0:T(8,128)} %param.4), kind=kOutput, calls=%fused_computation.108 | convolution fusion | flops 18874368 | bytes 6352896 | tf_op jit(solution)/shard_map/tkij,tkj->ti/dot_general | solution.py:96
  258.4 5.1 %fusion.67 = f32[24,1,2,256]{3,1,2,0:T(1,128)S(1)} fusion(f32[24,128,1,1]{1,2,3,0:T(1,128)S(1)} %bitcast.68, f32[24,2,128,256]{3,2,1,0:T(8,128)} %param.4), kind=kOutput, calls=%fused_computation.109 | convolution fusion | flops 18874368 | bytes 6352896 | tf_op jit(solution)/shard_map/tkij,ti->tkj/dot_general | solution.py:104
  263.9 4.2 %collective-permute-start.15 = (f32[48,256]{1,0:T(8,128)S(1)}, f32[48,256]{1,0:T(8,128)S(1)}, u32[]{:S(2)}, u32[]{:S(2)}) collective-permute-start(f32[48,256]{1,0:T(8,128)S(1)} %get-tuple-element.60), channel_id=1, source_target_pairs={{0,4},{4,8},{8,12},{12,16},{16,20},{20,24},{24,28},{28,32},{32,36}... | collective-permute-start | bytes 147464 | tf_op jit(solution)/shard_map/ppermute | solution.py:50
  268.2 1.9 collective-permute-start.14
  270.1 3.5 collective-permute-done.14
  273.6 6.8 %all_to_all.50 = f32[4,12,256]{2,1,0:T(8,128)S(1)} all-to-all(f32[4,12,256]{2,1,0:T(8,128)S(1)} %reshape.119), channel_id=1, replica_groups=mesh['slab_0'=8,'slab_1'=4,'slab_2'=2,'sub'=4] {'sub'}, dimensions={0} | all-to-all | bytes 98304 | tf_op jit(solution)/shard_map/all_to_all | solution.py:60
  281.1 13.9 %all-reduce = (f32[]{:T(128)}, f32[]{:T(128)}, f32[]{:T(128)}) all-reduce(f32[]{:T(128)} %get-tuple-element.49, f32[]{:T(128)} %get-tuple-element.3, f32[]{:T(128)} %get-tuple-element.2), channel_id=1, replica_groups=mesh['slab_0'=8,'slab_1'=4,'slab_2'=2,'sub'=4] {'slab_0'}, use_global_device_ids=true, to_apply=%region_40.41 | all-reduce | flops 3 | bytes 24 | tf_op jit(solution)/shard_map/psum | solution.py:65
  295.0 13.6 %all-reduce.6 = (f32[]{:T(128)}, f32[]{:T(128)}, f32[]{:T(128)}) all-reduce(f32[]{:T(128)} %get-tuple-element.9, f32[]{:T(128)} %get-tuple-element.10, f32[]{:T(128)} %get-tuple-element.11), channel_id=1, replica_groups=mesh['slab_0'=8,'slab_1'=4,'slab_2'=2,'sub'=4] {'slab_1'}, use_global_device_ids=true, to_apply=%region_41.42 | all-reduce | flops 3 | bytes 24 | tf_op jit(solution)/shard_map/psum | solution.py:65
  308.5 4.8 %all-reduce.9 = (f32[]{:T(128)}, f32[]{:T(128)}, f32[]{:T(128)}) all-reduce(f32[]{:T(128)} %get-tuple-element.29, f32[]{:T(128)} %get-tuple-element.30, f32[]{:T(128)} %get-tuple-element.31), channel_id=1, replica_groups=mesh['slab_0'=8,'slab_1'=4,'slab_2'=2,'sub'=4] {'slab_2'}, use_global_device_ids=true, to_apply=%region_42.43 | all-reduce | flops 3 | bytes 24 | tf_op jit(solution)/shard_map/psum | solution.py:65
  313.3 7.5 %all-reduce.3 = (f32[]{:T(128)}, f32[]{:T(128)}, f32[]{:T(128)}) all-reduce(f32[]{:T(128)} %get-tuple-element.39, f32[]{:T(128)} %get-tuple-element.40, f32[]{:T(128)} %get-tuple-element.41), channel_id=1, replica_groups=mesh['slab_0'=8,'slab_1'=4,'slab_2'=2,'sub'=4] {'sub'}, use_global_device_ids=true, to_apply=%region_43.44 | all-reduce | flops 3 | bytes 24 | tf_op jit(solution)/shard_map/psum | solution.py:65
  322.8 6.8 %all_to_all.51 = f32[4,12,256]{2,1,0:T(8,128)S(1)} all-to-all(f32[4,12,256]{2,1,0:T(8,128)S(1)} %broadcast_in_dim.22), channel_id=1, replica_groups=mesh['slab_0'=8,'slab_1'=4,'slab_2'=2,'sub'=4] {'sub'}, dimensions={0} | all-to-all | bytes 98304 | tf_op jit(solution)/shard_map/all_to_all | solution.py:20
  329.7 5.4 %collective-permute-start.17 = (f32[48,256]{1,0:T(8,128)S(1)}, f32[48,256]{1,0:T(8,128)S(1)}, u32[]{:S(2)}, u32[]{:S(2)}) collective-permute-start(f32[48,256]{1,0:T(8,128)S(1)} %reshape.120), channel_id=1, source_target_pairs={{4,0},{8,4},{12,8},{16,12},{20,16},{24,20},{28,24},{32,28},{36,32}... | collective-permute-start | bytes 147464 | tf_op jit(solution)/shard_map/ppermute | solution.py:42
  335.1 3.8 collective-permute-start.16
  338.9 0.9 collective-permute-done.16
  340.1 7.3 %fusion.68 = f32[24,1,128,1]{2,1,3,0:T(1,128)S(1)} fusion(f32[24,2,256,1]{2,3,1,0:T(1,128)S(1)} %reshape.147, f32[24,2,128,256]{3,2,1,0:T(8,128)} %param.4), kind=kOutput, calls=%fused_computation.110 | convolution fusion | flops 18874368 | bytes 6352896 | tf_op jit(solution)/shard_map/tkij,tkj->ti/dot_general | solution.py:96
  348.0 13.5 %psum.348 = f32[]{:T(128)} all-reduce(f32[]{:T(128)} %multiply_reduce_fusion.5), channel_id=1, replica_groups=mesh['slab_0'=8,'slab_1'=4,'slab_2'=2,'sub'=4] {'slab_0'}, use_global_device_ids=true, to_apply=%region_56.57 | all-reduce | flops 1 | bytes 8 | tf_op jit(solution)/shard_map/psum | solution.py:65
  361.5 7.3 %psum.349 = f32[]{:T(128)} all-reduce(f32[]{:T(128)} %psum.348), channel_id=1, replica_groups=mesh['slab_0'=8,'slab_1'=4,'slab_2'=2,'sub'=4] {'slab_1'}, use_global_device_ids=true, to_apply=%region_57.58 | all-reduce | flops 1 | bytes 8 | tf_op jit(solution)/shard_map/psum | solution.py:65
  368.8 10.3 %psum.350 = f32[]{:T(128)} all-reduce(f32[]{:T(128)} %psum.349), channel_id=1, replica_groups=mesh['slab_0'=8,'slab_1'=4,'slab_2'=2,'sub'=4] {'slab_2'}, use_global_device_ids=true, to_apply=%region_58.59 | all-reduce | flops 1 | bytes 8 | tf_op jit(solution)/shard_map/psum | solution.py:65
  379.2 7.5 %psum.351 = f32[]{:T(128)} all-reduce(f32[]{:T(128)} %psum.350), channel_id=1, replica_groups=mesh['slab_0'=8,'slab_1'=4,'slab_2'=2,'sub'=4] {'sub'}, use_global_device_ids=true, to_apply=%region_59.60 | all-reduce | flops 1 | bytes 8 | tf_op jit(solution)/shard_map/psum | solution.py:65
  (81 shorter events, 9.5 us)
Async XLA Ops:
  0.6 6.6 %copy-start.1 = (s32[24,2]{0,1:T(2,128)S(1)}, s32[24,2]{0,1:T(2,128)}, u32[]{:S(2)}) copy-start(s32[24,2]{0,1:T(2,128)} %param.5) | copy-start | bytes 580
  7.8 16.1 %collective-permute-start.1 = (f32[48,256]{1,0:T(8,128)S(1)}, f32[48,256]{1,0:T(8,128)S(1)}, u32[]{:S(2)}, u32[]{:S(2)}) collective-permute-start(f32[48,256]{1,0:T(8,128)S(1)} %get-tuple-element.68), channel_id=1, source_target_pairs={{0,4},{4,8},{8,12},{12,16},{16,20},{20,24},{24,28},{28,32},{32,36}... | collective-permute-start | bytes 147464 | tf_op jit(solution)/shard_map/ppermute | solution.py:50
  12.3 11.6 %collective-permute-start = (f32[48,256]{1,0:T(8,128)S(1)}, f32[48,256]{1,0:T(8,128)S(1)}, u32[]{:S(2)}, u32[]{:S(2)}) collective-permute-start(f32[48,256]{1,0:T(8,128)S(1)} %get-tuple-element.67), channel_id=1, source_target_pairs={{4,0},{8,4},{12,8},{16,12},{20,16},{24,20},{28,24},{32,28},{36,32}... | collective-permute-start | bytes 147464 | tf_op jit(solution)/shard_map/ppermute | solution.py:50
  18.4 10.4 %collective-permute-start.3 = (f32[48,256]{1,0:T(8,128)S(1)}, f32[48,256]{1,0:T(8,128)S(1)}, u32[]{:S(2)}, u32[]{:S(2)}) collective-permute-start(f32[48,256]{1,0:T(8,128)S(1)} %get-tuple-element.66), channel_id=1, source_target_pairs={{0,4},{4,8},{8,12},{12,16},{16,20},{20,24},{24,28},{28,32},{32,36}... | collective-permute-start | bytes 147464 | tf_op jit(solution)/shard_map/ppermute | solution.py:50
  22.0 6.8 %collective-permute-start.2 = (f32[48,256]{1,0:T(8,128)S(1)}, f32[48,256]{1,0:T(8,128)S(1)}, u32[]{:S(2)}, u32[]{:S(2)}) collective-permute-start(f32[48,256]{1,0:T(8,128)S(1)} %get-tuple-element.65), channel_id=1, source_target_pairs={{4,0},{8,4},{12,8},{16,12},{20,16},{24,20},{28,24},{32,28},{36,32}... | collective-permute-start | bytes 147464 | tf_op jit(solution)/shard_map/ppermute | solution.py:50
  24.6 8.7 %all-to-all-start = ((f32[4,12,256]{2,1,0:T(8,128)}), f32[4,12,256]{2,1,0:T(8,128)S(1)}, u32[]{:S(2)}, u32[]{:S(2)}) async-start(f32[4,12,256]{2,1,0:T(8,128)} %reshape.105), calls=%async_computation | async-start | bytes 131072 | tf_op jit(solution)/shard_map/all_to_all | solution.py:60
  33.3 8.3 %all-to-all-start.1 = ((f32[4,12,256]{2,1,0:T(8,128)}), f32[4,12,256]{2,1,0:T(8,128)S(1)}, u32[]{:S(2)}, u32[]{:S(2)}) async-start(f32[4,12,256]{2,1,0:T(8,128)} %reshape.107), calls=%async_computation.1 | async-start | bytes 131072 | tf_op jit(solution)/shard_map/all_to_all | solution.py:60
  48.5 8.7 %collective-permute-start.5 = (f32[48,256]{1,0:T(8,128)S(1)}, f32[48,256]{1,0:T(8,128)S(1)}, u32[]{:S(2)}, u32[]{:S(2)}) collective-permute-start(f32[48,256]{1,0:T(8,128)S(1)} %reshape.108), channel_id=1, source_target_pairs={{4,0},{8,4},{12,8},{16,12},{20,16},{24,20},{28,24},{32,28},{36,32}... | collective-permute-start | bytes 147464 | tf_op jit(solution)/shard_map/ppermute | solution.py:42
  52.0 6.4 %collective-permute-start.4 = (f32[48,256]{1,0:T(8,128)S(1)}, f32[48,256]{1,0:T(8,128)S(1)}, u32[]{:S(2)}, u32[]{:S(2)}) collective-permute-start(f32[48,256]{1,0:T(8,128)S(1)} %reshape.108), channel_id=1, source_target_pairs={{0,4},{4,8},{8,12},{12,16},{16,20},{20,24},{24,28},{28,32},{32,36}... | collective-permute-start | bytes 147464 | tf_op jit(solution)/shard_map/ppermute | solution.py:39
  72.1 6.2 %collective-permute-start.7 = (f32[48,256]{1,0:T(8,128)S(1)}, f32[48,256]{1,0:T(8,128)S(1)}, u32[]{:S(2)}, u32[]{:S(2)}) collective-permute-start(f32[48,256]{1,0:T(8,128)S(1)} %get-tuple-element.64), channel_id=1, source_target_pairs={{0,4},{4,8},{8,12},{12,16},{16,20},{20,24},{24,28},{28,32},{32,36}... | collective-permute-start | bytes 147464 | tf_op jit(solution)/shard_map/ppermute | solution.py:50
  76.3 5.4 %collective-permute-start.6 = (f32[48,256]{1,0:T(8,128)S(1)}, f32[48,256]{1,0:T(8,128)S(1)}, u32[]{:S(2)}, u32[]{:S(2)}) collective-permute-start(f32[48,256]{1,0:T(8,128)S(1)} %get-tuple-element.63), channel_id=1, source_target_pairs={{4,0},{8,4},{12,8},{16,12},{20,16},{24,20},{28,24},{32,28},{36,32}... | collective-permute-start | bytes 147464 | tf_op jit(solution)/shard_map/ppermute | solution.py:50
  149.8 9.1 %collective-permute-start.9 = (f32[48,256]{1,0:T(8,128)S(1)}, f32[48,256]{1,0:T(8,128)S(1)}, u32[]{:S(2)}, u32[]{:S(2)}) collective-permute-start(f32[48,256]{1,0:T(8,128)S(1)} %reshape.112), channel_id=1, source_target_pairs={{4,0},{8,4},{12,8},{16,12},{20,16},{24,20},{28,24},{32,28},{36,32}... | collective-permute-start | bytes 147464 | tf_op jit(solution)/shard_map/ppermute | solution.py:42
  155.2 4.7 %collective-permute-start.8 = (f32[48,256]{1,0:T(8,128)S(1)}, f32[48,256]{1,0:T(8,128)S(1)}, u32[]{:S(2)}, u32[]{:S(2)}) collective-permute-start(f32[48,256]{1,0:T(8,128)S(1)} %reshape.112), channel_id=1, source_target_pairs={{0,4},{4,8},{8,12},{12,16},{16,20},{20,24},{24,28},{28,32},{32,36}... | collective-permute-start | bytes 147464 | tf_op jit(solution)/shard_map/ppermute | solution.py:39
  173.6 6.2 %collective-permute-start.11 = (f32[48,256]{1,0:T(8,128)S(1)}, f32[48,256]{1,0:T(8,128)S(1)}, u32[]{:S(2)}, u32[]{:S(2)}) collective-permute-start(f32[48,256]{1,0:T(8,128)S(1)} %get-tuple-element.62), channel_id=1, source_target_pairs={{0,4},{4,8},{8,12},{12,16},{16,20},{20,24},{24,28},{28,32},{32,36}... | collective-permute-start | bytes 147464 | tf_op jit(solution)/shard_map/ppermute | solution.py:50
  177.9 5.4 %collective-permute-start.10 = (f32[48,256]{1,0:T(8,128)S(1)}, f32[48,256]{1,0:T(8,128)S(1)}, u32[]{:S(2)}, u32[]{:S(2)}) collective-permute-start(f32[48,256]{1,0:T(8,128)S(1)} %get-tuple-element.61), channel_id=1, source_target_pairs={{4,0},{8,4},{12,8},{16,12},{20,16},{24,20},{28,24},{32,28},{36,32}... | collective-permute-start | bytes 147464 | tf_op jit(solution)/shard_map/ppermute | solution.py:50
  240.1 9.0 %collective-permute-start.13 = (f32[48,256]{1,0:T(8,128)S(1)}, f32[48,256]{1,0:T(8,128)S(1)}, u32[]{:S(2)}, u32[]{:S(2)}) collective-permute-start(f32[48,256]{1,0:T(8,128)S(1)} %reshape.116), channel_id=1, source_target_pairs={{4,0},{8,4},{12,8},{16,12},{20,16},{24,20},{28,24},{32,28},{36,32}... | collective-permute-start | bytes 147464 | tf_op jit(solution)/shard_map/ppermute | solution.py:42
  245.5 4.7 %collective-permute-start.12 = (f32[48,256]{1,0:T(8,128)S(1)}, f32[48,256]{1,0:T(8,128)S(1)}, u32[]{:S(2)}, u32[]{:S(2)}) collective-permute-start(f32[48,256]{1,0:T(8,128)S(1)} %reshape.116), channel_id=1, source_target_pairs={{0,4},{4,8},{8,12},{12,16},{16,20},{20,24},{24,28},{28,32},{32,36}... | collective-permute-start | bytes 147464 | tf_op jit(solution)/shard_map/ppermute | solution.py:39
  258.4 129.6 %copy-start = (f32[24,128]{1,0:T(8,128)S(1)}, f32[24,128]{1,0:T(8,128)}, u32[]{:S(2)}) copy-start(f32[24,128]{1,0:T(8,128)} %param.7) | copy-start | bytes 36868
  263.9 6.2 %collective-permute-start.15 = (f32[48,256]{1,0:T(8,128)S(1)}, f32[48,256]{1,0:T(8,128)S(1)}, u32[]{:S(2)}, u32[]{:S(2)}) collective-permute-start(f32[48,256]{1,0:T(8,128)S(1)} %get-tuple-element.60), channel_id=1, source_target_pairs={{0,4},{4,8},{8,12},{12,16},{16,20},{20,24},{24,28},{28,32},{32,36}... | collective-permute-start | bytes 147464 | tf_op jit(solution)/shard_map/ppermute | solution.py:50
  268.2 5.4 %collective-permute-start.14 = (f32[48,256]{1,0:T(8,128)S(1)}, f32[48,256]{1,0:T(8,128)S(1)}, u32[]{:S(2)}, u32[]{:S(2)}) collective-permute-start(f32[48,256]{1,0:T(8,128)S(1)} %get-tuple-element.59), channel_id=1, source_target_pairs={{4,0},{8,4},{12,8},{16,12},{20,16},{24,20},{28,24},{32,28},{36,32}... | collective-permute-start | bytes 147464 | tf_op jit(solution)/shard_map/ppermute | solution.py:50
  329.7 9.2 %collective-permute-start.17 = (f32[48,256]{1,0:T(8,128)S(1)}, f32[48,256]{1,0:T(8,128)S(1)}, u32[]{:S(2)}, u32[]{:S(2)}) collective-permute-start(f32[48,256]{1,0:T(8,128)S(1)} %reshape.120), channel_id=1, source_target_pairs={{4,0},{8,4},{12,8},{16,12},{20,16},{24,20},{28,24},{32,28},{36,32}... | collective-permute-start | bytes 147464 | tf_op jit(solution)/shard_map/ppermute | solution.py:42
  335.1 4.7 %collective-permute-start.16 = (f32[48,256]{1,0:T(8,128)S(1)}, f32[48,256]{1,0:T(8,128)S(1)}, u32[]{:S(2)}, u32[]{:S(2)}) collective-permute-start(f32[48,256]{1,0:T(8,128)S(1)} %reshape.120), channel_id=1, source_target_pairs={{0,4},{4,8},{8,12},{12,16},{16,20},{20,24},{24,28},{28,32},{32,36}... | collective-permute-start | bytes 147464 | tf_op jit(solution)/shard_map/ppermute | solution.py:39
where the time goes:
time: 392 us; the launch traced here: 389 us
  blocking collectives  216 us (55%)
  starting transfers between devices  73.9 us (19%)
  matrix products  51.9 us (13%)
  waiting for transfers between devices  23.5 us (6%)
  other arithmetic  10.6 us (3%)
  between operations  10.4 us (3%)
    psum x16, blocking collectives, one_axis_at_a_time(): return functools.reduce(lax.psum, axes, value)  169 us
    ppermute x10, starting transfers between devices, from_behind(): return lax.ppermute(block, axis, route)  30.5 us
    dot_general x4, matrix products, forward(): image = jnp.einsum('tkij,tkj->ti', values, picked, precision=precise)  29 us
    all_to_all x4, blocking collectives, copy_for_each(): return lax.all_to_all(copies, axis, split_axis=0, concat_axis=0, tiled=True)  27.4 us
    all_to_all x3, blocking collectives, sent_and_summed(): lax.all_to_all(parts, axis, split_axis=0, concat_axis=0, tiled=True)  20.5 us
    dot_general x4, matrix products, backward(): jnp.einsum('tkij,ti->tkj', values, rows, precision=precise)  20.3 us
    ppermute x4, starting transfers between devices, with_halo(): lax.ppermute(lax.slice_in_dim(block, 0, width, axis=dim), axis, backward)  19.7 us
    ppermute x4, starting transfers between devices, with_halo(): lax.ppermute(lax.slice_in_dim(block, block.shape[dim] - width, None, axis...  16.2 us
  transfers between devices with their start and end apart: 20, of which 9 were waited for; matrix products, arithmetic and copies ran while one was open for 1% of the time, Pallas kernels for 0%

commit v1 on v0

v1 whole, which is shorter than its diff:
```python
import functools

import jax
import jax.numpy as jnp
from jax import lax
from jax.experimental import pallas as pl
from jax.experimental.pallas import tpu as pltpu
from jax.sharding import PartitionSpec as P

MESH = pl.DeviceIdType.MESH
NODES = 12
XGROUP = 8
CHUNKS = 4
F32 = jnp.float32
BF16 = jnp.bfloat16


def total(value):
    return jnp.sum(jnp.sum(value, axis=1, keepdims=True), axis=0, keepdims=True)


def packed(parts):
    lanes = lax.broadcasted_iota(jnp.int32, (1, 128), 1)
    row = jnp.zeros((1, 128), F32)
    for place, part in enumerate(parts):
        row = jnp.where(lanes == place, part, row)
    return row


def unpacked(row, count):
    lanes = lax.broadcasted_iota(jnp.int32, (1, 128), 1)
    return [
        jnp.sum(jnp.where(lanes == place, row, 0.0), axis=1, keepdims=True) for place in range(count)
    ]


def kernel(
    slabs,
    subs,
    xgroup,
    ids_ref,
    count_ref,
    values_hbm,
    side_ref,
    solution_ref,
    residual_ref,
    values,
    ids_buf,
    first_terms,
    terms,
    first_sums,
    sums,
    first_near,
    first_far,
    near,
    far,
    window,
    rows,
    xred,
    zred,
    yred,
    load_sem,
    ids_send,
    ids_recv,
    term_send,
    term_recv,
    sum_send,
    sum_recv,
    x_send,
    x_recv,
    z_send,
    z_recv,
    y_send,
    y_recv,
):
    tiles = values.shape[0]
    width = values.shape[3]
    own = 2 * tiles
    nodes = subs * NODES
    slab = lax.axis_index("slab")
    sub = lax.axis_index("sub")
    zgroup = slabs // xgroup
    x_place = lax.rem(slab, xgroup)
    z_place = slab // xgroup

    def sub_peer(step):
        return (slab, lax.rem(sub + step, subs))

    def slab_peer(step):
        return (lax.rem(slab + step + slabs, slabs), sub)

    def x_peer(step):
        return (z_place * xgroup + lax.rem(x_place + step, xgroup), sub)

    def z_peer(step):
        return (lax.rem(z_place + step, zgroup) * xgroup + x_place, sub)

    chunk = tiles // CHUNKS
    loads = [
        pltpu.make_async_copy(
            values_hbm.at[pl.ds(part * chunk, chunk)],
            values.at[pl.ds(part * chunk, chunk)],
            load_sem.at[part],
        )
        for part in range(CHUNKS)
    ]
    for load in loads:
        load.start()

    barrier = pltpu.get_barrier_semaphore()
    partners = (
        [sub_peer(step) for step in range(1, subs)]
        + [slab_peer(step) for step in (-2, -1, 1, 2)]
        + [x_peer(step) for step in range(1, xgroup)]
        + [z_peer(step) for step in range(1, zgroup)]
    )
    for partner in partners:
        pl.semaphore_signal(barrier, inc=1, device_id=partner, device_id_type=MESH)

    base = (slab - 1) * nodes
    count = count_ref[0, 0]
    lanes = lax.broadcasted_iota(jnp.int32, (1, 256), 1)
    ids_row = jnp.zeros((1, 256), jnp.int32)
    for tile in range(tiles):
        for slot in range(2):
            mark = ids_ref[tile, slot] - base + 1
            ids_row = jnp.where(lanes == sub * own + 2 * tile + slot, mark, ids_row)
    ids_buf[sub] = ids_row

    live_rows = lax.broadcasted_iota(jnp.int32, (tiles, 128), 0) < count
    residual = jnp.where(live_rows, side_ref[...], 0.0)
    rows[...] = residual
    eye = lax.broadcasted_iota(jnp.int32, (128, 128), 0) == lax.broadcasted_iota(
        jnp.int32, (128, 128), 1
    )

    def copy(source, target, send, recv, peer):
        return pltpu.make_async_remote_copy(
            src_ref=source,
            dst_ref=target,
            send_sem=send,
            recv_sem=recv,
            device_id=peer,
            device_id_type=MESH,
        )

    def live_of(tile):
        return jnp.where(tile < count, 1.0, 0.0).astype(F32)

    def first_tile(tile):
        live = live_of(tile)
        column = jnp.sum(
            jnp.where(eye, rows[pl.ds(tile, 1), :], 0.0), axis=1, keepdims=True
        )
        for slot in range(2):
            block = values[tile, slot]
            at = sub * own + 2 * tile + slot
            first_terms[0, pl.ds(at, 1), :] = jnp.sum(block * column, axis=0, keepdims=True)
            first_terms[1, pl.ds(at, 1), :] = jnp.sum(block * block, axis=0, keepdims=True) * live

    def picked(tile, slot):
        at = jnp.minimum(jnp.maximum(ids_ref[tile, slot] - base, 0), 3 * nodes - 1)
        return window[pl.ds(at, 1), :]

    def image_of(tile):
        live = live_of(tile)
        low = picked(tile, 0) * live
        high = picked(tile, 1) * live
        product = values[tile, 0] * low + values[tile, 1] * high
        folded = sum(product[:, 128 * i : 128 * (i + 1)] for i in range(width // 128))
        column = jnp.sum(folded, axis=1, keepdims=True)
        rows[pl.ds(tile, 1), :] = jnp.sum(jnp.where(eye, column, 0.0), axis=0, keepdims=True)
        return column

    def full_tile(step, tile):
        column = image_of(tile)
        for slot in range(2):
            at = sub * own + 2 * tile + slot
            terms[step, pl.ds(at, 1), :] = jnp.sum(
                values[tile, slot] * column, axis=0, keepdims=True
            )

    def wait_barrier():
        pl.semaphore_wait(barrier, len(partners))

    def own_rows(ref, step):
        return ref.at[step, pl.ds(sub * own, own)]

    for part in range(CHUNKS):
        loads[part].wait()

        @pl.loop(part * chunk, (part + 1) * chunk, unroll=2)
        def _(tile):
            first_tile(tile)

    wait_barrier()
    sent = []
    for step in range(1, subs):
        place = lax.rem(sub, subs)
        peer = sub_peer(step)
        item = copy(ids_buf.at[sub], ids_buf.at[sub], ids_send.at[step], ids_recv.at[step], peer)
        item.start()
        sent.append(item)
        for part in range(2):
            item = copy(
                own_rows(first_terms, part),
                own_rows(first_terms, part),
                term_send.at[3 + part, step],
                term_recv.at[3 + part, step],
                peer,
            )
            item.start()
            sent.append(item)
    for item in sent:
        item.wait_recv()

    all_ids = sum(ids_buf[i] for i in range(subs))[:, : subs * own]
    row_ids = lax.broadcasted_iota(jnp.int32, (3 * nodes, subs * own), 0) + 1
    selector = jnp.where(row_ids == all_ids, 1.0, 0.0).astype(BF16)

    def summed(value):
        high = value.astype(BF16)
        rest = value - high.astype(F32)
        middle = rest.astype(BF16)
        low = (rest - middle.astype(F32)).astype(BF16)
        return sum(
            jnp.dot(selector, piece, preferred_element_type=F32) for piece in (high, middle, low)
        )

    def exchange(sum_ref, near_ref, far_ref, index):
        moves = (
            (1, pl.ds(nodes, 2 * nodes), near_ref.at[0]),
            (-1, pl.ds(0, 2 * nodes), near_ref.at[1]),
            (2, pl.ds(2 * nodes, nodes), far_ref.at[0]),
            (-2, pl.ds(0, nodes), far_ref.at[1]),
        )
        items = []
        for place, (step, part, target) in enumerate(moves):
            item = copy(
                sum_ref.at[part],
                target,
                sum_send.at[index, place],
                sum_recv.at[index, place],
                slab_peer(step),
            )
            item.start()
            items.append(item)
        return items

    def combined(mine, near_ref, far_ref):
        below, above = near_ref[0], near_ref[1]
        return jnp.concatenate(
            [
                (far_ref[0] + below[:nodes]) + mine[:nodes],
                (below[nodes:] + mine[nodes : 2 * nodes]) + above[:nodes],
                (mine[2 * nodes :] + above[nodes:]) + far_ref[1],
            ],
            axis=0,
        )

    mine = []
    for part in range(2):
        mine.append(summed(first_terms[part]))
        first_sums[part] = mine[part]
        sent += exchange(first_sums.at[part], first_near.at[part], first_far.at[part], 3 + part)
    for item in sent[-8:]:
        item.wait_recv()
    normal = combined(mine[0], first_near.at[0], first_far.at[0])
    squares = combined(mine[1], first_near.at[1], first_far.at[1])
    jacobi = 1.0 / (1.0 + squares)

    def middle_of(value):
        return value[nodes : 2 * nodes]

    def start_x(index, row):
        xred[index, x_place] = row
        items = []
        for step in range(1, xgroup):
            item = copy(
                xred.at[index, x_place],
                xred.at[index, x_place],
                x_send.at[index, step],
                x_recv.at[index, step],
                x_peer(step),
            )
            item.start()
            items.append(item)
        return items

    def turn_to_z(index, items):
        for item in items:
            item.wait_recv()
        row = jnp.sum(xred[index], axis=0)
        zred[index, z_place] = row
        later = []
        for step in range(1, zgroup):
            item = copy(
                zred.at[index, z_place],
                zred.at[index, z_place],
                z_send.at[index, step],
                z_recv.at[index, step],
                z_peer(step),
            )
            item.start()
            later.append(item)
        return later

    def finish_z(index, items):
        for item in items:
            item.wait_recv()
        return jnp.sum(zred[index], axis=0)

    def applied(step, pending):
        @pl.loop(0, tiles, unroll=4)
        def _(tile):
            full_tile(step, tile)

        items = []
        for peer_step in range(1, subs):
            item = copy(
                own_rows(terms, step),
                own_rows(terms, step),
                term_send.at[step, peer_step],
                term_recv.at[step, peer_step],
                sub_peer(peer_step),
            )
            item.start()
            items.append(item)
        later = []
        if pending is not None:
            later = turn_to_z(*pending)
        for item in items:
            item.wait_recv()
        here = summed(terms[step])
        sums[step] = here
        moved = exchange(sums.at[step], near.at[step], far.at[step], step)
        for item in moved:
            item.wait_recv()
        sent.extend(items + later + moved)
        return combined(here, near.at[step], far.at[step]), later

    u_all = jacobi * normal
    window[...] = u_all
    w_all, _ = applied(0, None)
    a_row = rows[...]
    r, u = middle_of(normal), middle_of(u_all)
    w = middle_of(w_all)
    items = start_x(0, packed([total(r * u), total(w * u)]))
    sent += items
    m_all = jacobi * w_all
    window[...] = m_all

    n_all, later = applied(1, (0, items))
    g_row = rows[...]
    rho_0, norm_0 = unpacked(finish_z(0, later), 2)
    alpha = rho_0 / norm_0
    z_all = n_all
    q, s, p = middle_of(m_all), w, u
    ap_row, aq_row = a_row, g_row
    w_all = w_all - alpha * z_all
    m_all = jacobi * w_all
    window[...] = m_all
    x = alpha * p
    r = r - alpha * s
    u = u - alpha * q
    residual = residual - alpha * ap_row
    a_row = a_row - alpha * aq_row
    w = middle_of(w_all)
    items = start_x(1, packed([total(r * u), total(w * u), total(w * p)]))
    sent += items

    n_all, later = applied(2, (1, items))
    g_row = rows[...]
    rho_1, uu, cross = unpacked(finish_z(1, later), 3)
    beta = rho_1 / rho_0
    norm_1 = uu + 2.0 * beta * cross + beta * beta * norm_0
    alpha = rho_1 / norm_1
    z_all = n_all + beta * z_all
    m = middle_of(m_all)
    w_all = w_all - alpha * z_all
    q = m + beta * q
    s = w + beta * s
    p = u + beta * p
    m_all = jacobi * w_all
    window[...] = m_all
    x = x + alpha * p
    r = r - alpha * s
    u = u - alpha * q
    ap_row = a_row + beta * ap_row
    aq_row = g_row + beta * aq_row
    residual = residual - alpha * ap_row
    a_row = a_row - alpha * aq_row
    w, m = middle_of(w_all), middle_of(m_all)

    @pl.loop(0, tiles, unroll=4)
    def _(tile):
        image_of(tile)

    g_row = rows[...]
    fields = [a_row, g_row, aq_row, ap_row]
    pairs = [(i, j) for i in range(4) for j in range(i, 4)]
    row_part = packed([total(fields[i] * fields[j]) for i, j in pairs])
    node_dots = [
        total(r * u),
        total(w * u),
        total(w * p),
        total(s * u),
        total(w * m),
        total(s * m),
        total(s * q),
    ]
    place = lax.broadcasted_iota(jnp.int32, (1, 128), 1)
    node_part = jnp.zeros((1, 128), F32)
    for index, part in enumerate(node_dots):
        node_part = jnp.where(place == len(pairs) + index, part, node_part)
    yred[sub] = row_part
    items = []
    for step in range(1, subs):
        item = copy(
            yred.at[sub], yred.at[sub], y_send.at[step], y_recv.at[step], sub_peer(step)
        )
        item.start()
        items.append(item)
    sent += items
    for item in items:
        item.wait_recv()
    items = start_x(2, jnp.sum(yred[...], axis=0) + node_part)
    sent += items
    later = turn_to_z(2, items)
    sent += later
    found = unpacked(finish_z(2, later), len(pairs) + len(node_dots))
    gram = dict(zip(pairs, found[: len(pairs)]))
    rho_2, uu, cross, s_u, w_m, s_m, s_q = found[len(pairs) :]
    beta = rho_2 / rho_1
    norm_2 = uu + 2.0 * beta * cross + beta * beta * norm_1
    alpha = rho_2 / norm_2
    rho_3 = (
        rho_2
        - 2.0 * alpha * (uu + beta * s_u)
        + alpha * alpha * (w_m + 2.0 * beta * s_m + beta * beta * s_q)
    )
    beta_3 = rho_3 / rho_2
    weights = [1.0 + beta_3, -alpha, -alpha * beta, beta_3 * beta]
    norm_3 = 0.0
    for i, j in pairs:
        norm_3 = norm_3 + (1.0 if i == j else 2.0) * weights[i] * weights[j] * gram[i, j]
    alpha_3 = rho_3 / norm_3
    p = u + beta * p
    x = x + alpha * p
    u = u - alpha * (m + beta * q)
    p = u + beta_3 * p
    x = x + alpha_3 * p
    ap_row = a_row + beta * ap_row
    last_row = sum(weights[i] * fields[i] for i in range(4))
    residual = residual - alpha * ap_row - alpha_3 * last_row
    residual_ref[...] = residual
    mine = x[:NODES]
    for index in range(1, subs):
        mine = jnp.where(sub == index, x[index * NODES : (index + 1) * NODES], mine)
    solution_ref[...] = mine
    for item in sent:
        item.wait_send()


def per_device(slabs, subs, values, block_ids, tile_counts, right_side):
    tiles, coupled, height, width = values.shape
    own = 2 * tiles
    nodes = subs * NODES
    xgroup = min(XGROUP, slabs // 2)
    zgroup = slabs // xgroup
    vmem = pltpu.VMEM
    dma = pltpu.SemaphoreType.DMA
    return pl.pallas_call(
        functools.partial(kernel, slabs, subs, xgroup),
        out_shape=(
            jax.ShapeDtypeStruct((NODES, width), F32),
            jax.ShapeDtypeStruct((tiles, height), F32),
        ),
        in_specs=[
            pl.BlockSpec(memory_space=pltpu.SMEM),
            pl.BlockSpec(memory_space=pltpu.SMEM),
            pl.BlockSpec(memory_space=pl.ANY),
            pl.BlockSpec(memory_space=pltpu.VMEM),
        ],
        out_specs=(
            pl.BlockSpec(memory_space=pltpu.VMEM),
            pl.BlockSpec(memory_space=pltpu.VMEM),
        ),
        scratch_shapes=[
            vmem(values.shape, F32),
            vmem((subs, 1, 256), jnp.int32),
            vmem((2, subs * own, width), F32),
            vmem((3, subs * own, width), F32),
            vmem((2, 3 * nodes, width), F32),
            vmem((3, 3 * nodes, width), F32),
            vmem((2, 2, 2 * nodes, width), F32),
            vmem((2, 2, nodes, width), F32),
            vmem((3, 2, 2 * nodes, width), F32),
            vmem((3, 2, nodes, width), F32),
            vmem((3 * nodes, width), F32),
            vmem((tiles, height), F32),
            vmem((3, xgroup, 1, 128), F32),
            vmem((3, zgroup, 1, 128), F32),
            vmem((subs, 1, 128), F32),
            dma((CHUNKS,)),
            dma((subs,)),
            dma((subs,)),
            dma((5, subs)),
            dma((5, subs)),
            dma((5, 4)),
            dma((5, 4)),
            dma((3, xgroup)),
            dma((3, xgroup)),
            dma((3, zgroup)),
            dma((3, zgroup)),
            dma((subs,)),
            dma((subs,)),
        ],
        compiler_params=pltpu.CompilerParams(
            collective_id=0, has_side_effects=True, vmem_limit_bytes=48 * 1024 * 1024
        ),
        name="cgls",
    )(block_ids, tile_counts, values, right_side)


def solution(mesh):
    both = ("slab", "sub")
    return jax.shard_map(
        functools.partial(per_device, mesh.shape["slab"], mesh.shape["sub"]),
        mesh=mesh,
        in_specs=(P(both, None, None, None), P(both, None), P("slab", "sub"), P(both, None)),
        out_specs=(P(both, None), P(both, None)),
        check_vma=False,
    )
```

time: 392 us -> 76.3 us (0.19)
  blocking collectives: 216 us -> 0 us
  starting transfers between devices: 73.9 us -> 0 us
  Pallas kernels: 0 us -> 72.2 us
  matrix products: 51.9 us -> 0 us
  waiting for transfers between devices: 23.5 us -> 0 us
  other arithmetic: 10.6 us -> 0 us
  between operations: 10.4 us -> 1.29 us
    psum x16 -> x0, blocking collectives: 169 us -> none  [one_axis_at_a_time(): return functools.reduce(lax.psum, axes, value)]
    pallas_call x0 -> x1, Pallas kernels: none -> 72.2 us  [per_device(): pl.pallas_call(functools.partial(kernel, slabs, subs, xgroup), out_shape=...]
    ppermute x18 -> x0, starting transfers between devices: 66.4 us -> none  [the longest x10 30.5 us: from_behind(): return lax.ppermute(block, axis, route)]
    dot_general x17 -> x0, matrix products: 51.9 us -> none  [the longest x4 29 us: forward(): image = jnp.einsum('tkij,tkj->ti', values, picked, precision=precise)]
    all_to_all x7 -> x0, blocking collectives: 47.9 us -> none  [the longest x4 27.4 us: copy_for_each(): return lax.all_to_all(copies, axis, split_axis=0, concat_axis=0, tiled=True)]
    ppermute x18 -> x0, waiting for transfers between devices: 14.6 us -> none  [the longest x10 10.4 us: from_behind(): return lax.ppermute(block, axis, route)]
    all_to_all x2 -> x0, waiting for transfers between devices: 8.85 us -> none  [sent_and_summed(): lax.all_to_all(parts, axis, split_axis=0, concat_axis=0, tiled=True)]
    all_to_all x2 -> x0, starting transfers between devices: 7.47 us -> none  [sent_and_summed(): lax.all_to_all(parts, axis, split_axis=0, concat_axis=0, tiled=True)]
  transfers between devices with their start and end apart: 20 -> 0, of which waited for: 9 -> 0; matrix products, arithmetic and copies ran while one was open for 1% -> 0% of each run, Pallas kernels for 0% -> 0%
where the time goes in v1:
time: 76.3 us; the launch traced here: 76.1 us
  Pallas kernels  72.2 us (95%)
  local copies, waits for them, and re-layouts  2.67 us (3%)
  between operations  1.29 us (2%)
    pallas_call x1, Pallas kernels, per_device(): pl.pallas_call(functools.partial(kernel, slabs, subs, xgroup), out_shape=...  72.2 us
    unnamed x5, local copies, waits for them, and re-layouts  2.67 us

profile of v1, /device:TPU:1, one launch (start us, length us, event | category | flops | bytes accessed | tf_op | source)
XLA Modules:
  0.0 76.1 jit_solution(8681481267343809165)
XLA Ops:
  1.3 0.8 copy.6.ids_ref
  2.0 0.0 copy-start
  2.0 0.7 copy-done
  2.7 72.2 %cgls.1 = (f32[12,256]{1,0:T(8,128)S(1)}, f32[24,128]{1,0:T(8,128)S(1)}) custom-call(s32[24,2]{1,0:T(8,128)S(1)} %copy.6.ids_ref, s32[1,1]{1,0:T(1,128)S(6)} %copy.9.count_ref, f32[24,2,128,256]{3,2,1,0:T(8,128)} %values_hbm.1, f32[24,128]{1,0:T(8,128)S(1)} %copy-done), custom_call_target="tpu_custom_call" | custom-call | tf_op jit(solution)/shard_map/cgls/pallas_call | solution.py:473
  74.9 0.6 copy.10
  75.5 0.6 copy.11
Async XLA Ops:
  2.0 0.7 copy-start

commit v2 on v0

v2 whole, which is shorter than its diff:
```python
import functools

import jax
import jax.numpy as jnp
from jax import lax
from jax.experimental import pallas as pl
from jax.experimental.pallas import tpu as pltpu
from jax.sharding import PartitionSpec as P

MESH = pl.DeviceIdType.MESH
NODES = 12
CORES = 2
ALONG_X = 4
GROUPS = 3
F32 = jnp.float32
BF16 = jnp.bfloat16


def total(value):
    return jnp.sum(jnp.sum(value, axis=1, keepdims=True), axis=0, keepdims=True)


def packed(parts):
    lanes = lax.broadcasted_iota(jnp.int32, (1, 128), 1)
    row = jnp.zeros((1, 128), F32)
    for place, part in enumerate(parts):
        row = jnp.where(lanes == place, part, row)
    return row


def unpacked(row, count):
    lanes = lax.broadcasted_iota(jnp.int32, (1, 128), 1)
    return [
        jnp.sum(jnp.where(lanes == place, row, 0.0), axis=1, keepdims=True) for place in range(count)
    ]


def kernel(
    slabs,
    subs,
    along_x,
    ids_hbm,
    count_ref,
    values_hbm,
    side_hbm,
    solution_ref,
    residual_ref,
    values,
    side,
    ids_ref,
    columns,
    ids_buf,
    first_terms,
    terms,
    first_sums,
    sums,
    first_near,
    first_far,
    near,
    far,
    window,
    rows,
    plane,
    depth,
    load_sem,
    side_sem,
    index_sem,
    ids_send,
    ids_recv,
    term_send,
    term_recv,
    sum_send,
    sum_recv,
    plane_send,
    plane_recv,
    depth_send,
    depth_recv,
):
    tiles = values.shape[0]
    own = 2 * tiles
    nodes = subs * NODES
    slab = lax.axis_index("slab")
    sub = lax.axis_index("sub")
    along_z = slabs // (along_x * CORES)
    core = lax.rem(slab, CORES)
    x_at = lax.rem(slab // CORES, along_x)
    z_at = slab // (CORES * along_x)
    plane_count = along_x * subs
    depth_count = along_z * CORES
    plane_at = x_at * subs + sub
    depth_at = z_at * CORES + core

    def sub_peer(step):
        return (slab, lax.rem(sub + step, subs))

    def slab_peer(step):
        return (lax.rem(slab + step + slabs, slabs), sub)

    def plane_peer(step):
        at = lax.rem(plane_at + step, plane_count)
        return ((z_at * along_x + at // subs) * CORES + core, lax.rem(at, subs))

    def depth_peer(step):
        at = lax.rem(depth_at + step, depth_count)
        return ((at // CORES * along_x + x_at) * CORES + lax.rem(at, CORES), sub)

    def half_of(half):
        return pl.ds(128 * half, 128)

    group = tiles // GROUPS
    side_load = pltpu.make_async_copy(side_hbm, side, side_sem)
    side_load.start()
    ids_load = pltpu.make_async_copy(ids_hbm, ids_ref, index_sem)
    ids_load.start()
    loads = []
    for half in range(2):
        for part in range(GROUPS):
            at = (pl.ds(part * group, group), slice(None), slice(None), half_of(half))
            loads.append(
                pltpu.make_async_copy(
                    values_hbm.at[at], values.at[at], load_sem.at[half * GROUPS + part]
                )
            )
    for load in loads:
        load.start()

    barrier = pltpu.get_barrier_semaphore()
    partners = (
        [slab_peer(step) for step in (-2, -1, 1, 2)]
        + [plane_peer(step) for step in range(1, plane_count)]
        + [depth_peer(step) for step in range(1, depth_count)]
    )
    for partner in partners:
        pl.semaphore_signal(barrier, inc=1, device_id=partner, device_id_type=MESH)

    base = (slab - 1) * nodes
    count = count_ref[0, 0]
    ids_load.wait()
    lanes = lax.broadcasted_iota(jnp.int32, (1, 256), 1)
    ids_row = jnp.zeros((1, 256), jnp.int32)
    for tile in range(tiles):
        for slot in range(2):
            mark = ids_ref[slot, tile] - base + 1
            ids_row = jnp.where(lanes == sub * own + 2 * tile + slot, mark, ids_row)
    ids_buf[sub] = ids_row

    live_rows = lax.broadcasted_iota(jnp.int32, (tiles, 128), 0) < count
    side_load.wait()
    residual = jnp.where(live_rows, side[...], 0.0)
    rows[...] = residual
    eye = lax.broadcasted_iota(jnp.int32, (128, 128), 0) == lax.broadcasted_iota(
        jnp.int32, (128, 128), 1
    )
    sent = []

    def copy(source, target, send, recv, peer):
        item = pltpu.make_async_remote_copy(
            src_ref=source,
            dst_ref=target,
            send_sem=send,
            recv_sem=recv,
            device_id=peer,
            device_id_type=MESH,
        )
        item.start()
        sent.append(item)
        return item

    def live_of(tile):
        return jnp.where(tile < count, 1.0, 0.0).astype(F32)

    def place_of(tile, slot):
        return pl.ds(sub * own + 2 * tile + slot, 1)

    def first_tile(tile, half):
        live = live_of(tile)
        if half == 0:
            column = jnp.sum(
                jnp.where(eye, rows[pl.ds(tile, 1), :], 0.0), axis=1, keepdims=True
            )
            column = jnp.broadcast_to(column, (128, 128))
            columns[tile] = column
        else:
            column = columns[tile]
        for slot in range(2):
            block = values[tile, slot, :, 128 * half : 128 * (half + 1)]
            at = place_of(tile, slot)
            first_terms[half, 0, at, :] = jnp.sum(block * column, axis=0, keepdims=True)
            first_terms[half, 1, at, :] = jnp.sum(block * block, axis=0, keepdims=True) * live

    def image_of(tile):
        live = live_of(tile)
        product = None
        for slot in range(2):
            at = jnp.minimum(jnp.maximum(ids_ref[slot, tile] - base, 0), 3 * nodes - 1)
            for half in range(2):
                row = window[half, pl.ds(at, 1), :] * live
                part = values[tile, slot, :, 128 * half : 128 * (half + 1)] * row
                product = part if product is None else product + part
        column = jnp.sum(product, axis=1, keepdims=True)
        rows[pl.ds(tile, 1), :] = jnp.sum(jnp.where(eye, column, 0.0), axis=0, keepdims=True)
        return column

    def back_tile(phase, tile, half):
        if half == 0:
            column = jnp.broadcast_to(image_of(tile), (128, 128))
            columns[tile] = column
        else:
            column = columns[tile]
        for slot in range(2):
            block = values[tile, slot, :, 128 * half : 128 * (half + 1)]
            terms[phase, half, 0, place_of(tile, slot), :] = jnp.sum(
                block * column, axis=0, keepdims=True
            )

    def spread(terms_ref, phase, half):
        part = terms_ref.at[half, :, pl.ds(sub * own, own)]
        return [
            copy(
                part,
                part,
                term_send.at[phase, half, step],
                term_recv.at[phase, half, step],
                sub_peer(step),
            )
            for step in range(1, subs)
        ]

    def arrived(items):
        for item in items:
            item.wait_recv()

    def summed(value):
        high = value.astype(BF16)
        rest = value - high.astype(F32)
        middle = rest.astype(BF16)
        low = (rest - middle.astype(F32)).astype(BF16)
        return sum(
            jnp.dot(selector, piece, preferred_element_type=F32) for piece in (high, middle, low)
        )

    def exchange(terms_ref, sums_ref, near_ref, far_ref, phase, half):
        mine = []
        for index in range(terms_ref.shape[1]):
            mine.append(summed(terms_ref[half, index]))
            sums_ref[half, index] = mine[index]
        moves = (
            (1, pl.ds(nodes, 2 * nodes), near_ref.at[half, 0]),
            (-1, pl.ds(0, 2 * nodes), near_ref.at[half, 1]),
            (2, pl.ds(2 * nodes, nodes), far_ref.at[half, 0]),
            (-2, pl.ds(0, nodes), far_ref.at[half, 1]),
        )
        items = [
            copy(
                sums_ref.at[half, :, part],
                target,
                sum_send.at[phase, half, place],
                sum_recv.at[phase, half, place],
                slab_peer(step),
            )
            for place, (step, part, target) in enumerate(moves)
        ]
        return mine, items

    def combined(mine, near_ref, far_ref, half):
        found = []
        for index, value in enumerate(mine):
            below, above = near_ref[half, 0, index], near_ref[half, 1, index]
            found.append(
                jnp.concatenate(
                    [
                        (far_ref[half, 0, index] + below[:nodes]) + value[:nodes],
                        (below[nodes:] + value[nodes : 2 * nodes]) + above[:nodes],
                        (value[2 * nodes :] + above[nodes:]) + far_ref[half, 1, index],
                    ],
                    axis=0,
                )
            )
        return found

    def start_plane(index, row):
        plane[index, plane_at] = row
        at = plane.at[index, plane_at]
        return [
            copy(at, at, plane_send.at[index, step], plane_recv.at[index, step], plane_peer(step))
            for step in range(1, plane_count)
        ]

    def start_depth(index, items):
        arrived(items)
        depth[index, depth_at] = jnp.sum(plane[index], axis=0)
        at = depth.at[index, depth_at]
        return [
            copy(at, at, depth_send.at[index, step], depth_recv.at[index, step], depth_peer(step))
            for step in range(1, depth_count)
        ]

    def finish_depth(index, items, number):
        arrived(items)
        return unpacked(jnp.sum(depth[index], axis=0), number)

    def middle_of(halves):
        return [half[nodes : 2 * nodes] for half in halves]

    def dot(one, other):
        return total(one[0] * other[0] + one[1] * other[1]) * (1.0 / subs)

    items = []
    for half in range(2):
        for part in range(GROUPS):
            loads[half * GROUPS + part].wait()

            @pl.loop(part * group, (part + 1) * group, unroll=2)
            def _(tile):
                first_tile(tile, half)

        if half == 0:
            pl.semaphore_wait(barrier, len(partners))
            place = ids_buf.at[sub]
            ids_items = [
                copy(place, place, ids_send.at[step], ids_recv.at[step], sub_peer(step))
                for step in range(1, subs)
            ]
        items.append(spread(first_terms, 0, half))
    arrived(ids_items)
    all_ids = sum(ids_buf[i] for i in range(subs))[:, : subs * own]
    row_ids = lax.broadcasted_iota(jnp.int32, (3 * nodes, subs * own), 0) + 1
    selector = jnp.where(row_ids == all_ids, 1.0, 0.0).astype(BF16)
    moved = []
    for half in range(2):
        arrived(items[half])
        moved.append(exchange(first_terms, first_sums, first_near, first_far, 0, half))
    normal, jacobi, u_all = [], [], []
    for half in range(2):
        mine, items = moved[half]
        arrived(items)
        found, squares = combined(mine, first_near, first_far, half)
        normal.append(found)
        jacobi.append(1.0 / (1.0 + squares))
        u_all.append(jacobi[half] * found)
        window[half] = u_all[half]

    def applied(phase, dots):
        items = []
        for half in range(2):

            @pl.loop(0, tiles, unroll=4)
            def _(tile):
                back_tile(phase, tile, half)

            items.append(spread(terms.at[phase], 1 + phase, half))
        later = dots() if dots is not None else None
        moved = []
        for half in range(2):
            arrived(items[half])
            moved.append(
                exchange(
                    terms.at[phase],
                    sums.at[phase],
                    near.at[phase],
                    far.at[phase],
                    1 + phase,
                    half,
                )
            )
        return moved, later

    def result(phase, moved, half):
        mine, items = moved[half]
        arrived(items)
        return combined(mine, near.at[phase], far.at[phase], half)[0]

    r, u = middle_of(normal), middle_of(u_all)

    def dots_0():
        a_row = rows[...]
        return start_plane(0, packed([dot(r, u), total(a_row * a_row)]))

    moved, reducing = applied(0, dots_0)
    a_row = rows[...]
    w_all, m_all = [], []
    for half in range(2):
        w_all.append(result(0, moved, half))
        m_all.append(jacobi[half] * w_all[half])
        window[half] = m_all[half]
    w, m = middle_of(w_all), middle_of(m_all)

    def dots_1():
        g_row = rows[...]
        return start_plane(
            1, packed([dot(w, u), dot(w, m), total(a_row * g_row), total(g_row * g_row)])
        )

    reducing = start_depth(0, reducing)
    moved, later = applied(1, dots_1)
    g_row = rows[...]
    rho, norm = finish_depth(0, reducing, 2)
    reducing = start_depth(1, later)
    alpha = rho / norm
    z_all = []
    for half in range(2):
        z_all.append(result(1, moved, half))
        w_all[half] = w_all[half] - alpha * z_all[half]
        window[half] = jacobi[half] * w_all[half]
        m_all[half] = jacobi[half] * w_all[half]
    q, s, p = m, w, u
    ap_row, aq_row = a_row, g_row
    x = [alpha * one for one in p]
    u = [one - alpha * other for one, other in zip(u, q)]
    r = [one - alpha * other for one, other in zip(r, s)]
    residual = residual - alpha * ap_row
    a_row = a_row - alpha * aq_row
    w, m = middle_of(w_all), middle_of(m_all)
    old_rho, old_norm, old_alpha = rho, norm, alpha

    moved, _ = applied(2, None)
    g_row = rows[...]
    w_u, w_m, a_g, g_g = finish_depth(1, reducing, 4)
    rho = old_rho - 2.0 * old_alpha * w_u + old_alpha * old_alpha * w_m
    beta = rho / old_rho
    lead = 1.0 + beta
    norm = (
        lead * lead * old_norm
        - 2.0 * lead * old_alpha * a_g
        + old_alpha * old_alpha * g_g
    )
    alpha = rho / norm
    for half in range(2):
        z_all[half] = result(2, moved, half) + beta * z_all[half]
        w_all[half] = w_all[half] - alpha * z_all[half]
        window[half] = jacobi[half] * w_all[half]
    q = [one + beta * other for one, other in zip(m, q)]
    s = [one + beta * other for one, other in zip(w, s)]
    p = [one + beta * other for one, other in zip(u, p)]
    x = [one + alpha * other for one, other in zip(x, p)]
    r = [one - alpha * other for one, other in zip(r, s)]
    u = [one - alpha * other for one, other in zip(u, q)]
    ap_row = a_row + beta * ap_row
    aq_row = g_row + beta * aq_row
    residual = residual - alpha * ap_row
    a_row = a_row - alpha * aq_row
    w = middle_of(w_all)
    m = [window[half, pl.ds(nodes, nodes)] for half in range(2)]
    rho_1, norm_1 = rho, norm

    node_dots = [
        dot(r, u),
        dot(w, u),
        dot(w, p),
        dot(s, u),
        dot(w, m),
        dot(s, m),
        dot(s, q),
    ]

    @pl.loop(0, tiles, unroll=4)
    def _(tile):
        image_of(tile)

    g_row = rows[...]
    fields = [a_row, g_row, aq_row, ap_row]
    pairs = [(i, j) for i in range(4) for j in range(i, 4)]
    row_dots = [total(fields[i] * fields[j]) for i, j in pairs]
    later = start_depth(2, start_plane(2, packed(node_dots + row_dots)))
    found = finish_depth(2, later, len(node_dots) + len(pairs))
    rho_2, uu, cross, s_u, w_m, s_m, s_q = found[: len(node_dots)]
    gram = dict(zip(pairs, found[len(node_dots) :]))
    beta = rho_2 / rho_1
    norm_2 = uu + 2.0 * beta * cross + beta * beta * norm_1
    alpha = rho_2 / norm_2
    rho_3 = (
        rho_2
        - 2.0 * alpha * (uu + beta * s_u)
        + alpha * alpha * (w_m + 2.0 * beta * s_m + beta * beta * s_q)
    )
    beta_3 = rho_3 / rho_2
    weights = [1.0 + beta_3, -alpha, -alpha * beta, beta_3 * beta]
    norm_3 = 0.0
    for i, j in pairs:
        norm_3 = norm_3 + (1.0 if i == j else 2.0) * weights[i] * weights[j] * gram[i, j]
    alpha_3 = rho_3 / norm_3
    p = [one + beta * other for one, other in zip(u, p)]
    x = [one + alpha * other for one, other in zip(x, p)]
    u = [one - alpha * (other + beta * last) for one, other, last in zip(u, m, q)]
    p = [one + beta_3 * other for one, other in zip(u, p)]
    x = [one + alpha_3 * other for one, other in zip(x, p)]
    ap_row = a_row + beta * ap_row
    last_row = sum(weights[i] * fields[i] for i in range(4))
    residual_ref[...] = residual - alpha * ap_row - alpha_3 * last_row
    for half in range(2):
        mine = x[half][:NODES]
        for index in range(1, subs):
            mine = jnp.where(sub == index, x[half][index * NODES : (index + 1) * NODES], mine)
        solution_ref[:, 128 * half : 128 * (half + 1)] = mine
    for item in sent:
        item.wait_send()


def per_device(slabs, subs, values, block_ids, tile_counts, right_side):
    tiles, coupled, height, width = values.shape
    own = 2 * tiles
    nodes = subs * NODES
    along_x = min(ALONG_X, slabs // CORES)
    plane_count = along_x * subs
    depth_count = slabs // along_x
    half = width // 2
    vmem = pltpu.VMEM
    dma = pltpu.SemaphoreType.DMA
    return pl.pallas_call(
        functools.partial(kernel, slabs, subs, along_x),
        out_shape=(
            jax.ShapeDtypeStruct((NODES, width), F32),
            jax.ShapeDtypeStruct((tiles, height), F32),
        ),
        in_specs=[
            pl.BlockSpec(memory_space=pl.ANY),
            pl.BlockSpec(memory_space=pltpu.SMEM),
            pl.BlockSpec(memory_space=pl.ANY),
            pl.BlockSpec(memory_space=pl.ANY),
        ],
        out_specs=(
            pl.BlockSpec(memory_space=pltpu.VMEM),
            pl.BlockSpec(memory_space=pltpu.VMEM),
        ),
        scratch_shapes=[
            vmem(values.shape, F32),
            vmem((tiles, height), F32),
            pltpu.SMEM((2, tiles), jnp.int32),
            vmem((tiles, height, half), F32),
            vmem((subs, 1, 256), jnp.int32),
            vmem((2, 2, subs * own, half), F32),
            vmem((3, 2, 1, subs * own, half), F32),
            vmem((2, 2, 3 * nodes, half), F32),
            vmem((3, 2, 1, 3 * nodes, half), F32),
            vmem((2, 2, 2, 2 * nodes, half), F32),
            vmem((2, 2, 2, nodes, half), F32),
            vmem((3, 2, 2, 1, 2 * nodes, half), F32),
            vmem((3, 2, 2, 1, nodes, half), F32),
            vmem((2, 3 * nodes, half), F32),
            vmem((tiles, height), F32),
            vmem((3, plane_count, 1, 128), F32),
            vmem((3, depth_count, 1, 128), F32),
            dma((2 * GROUPS,)),
            dma,
            dma,
            dma((subs,)),
            dma((subs,)),
            dma((4, 2, subs)),
            dma((4, 2, subs)),
            dma((4, 2, 4)),
            dma((4, 2, 4)),
            dma((3, plane_count)),
            dma((3, plane_count)),
            dma((3, depth_count)),
            dma((3, depth_count)),
        ],
        compiler_params=pltpu.CompilerParams(
            collective_id=0, has_side_effects=True, vmem_limit_bytes=67043328
        ),
        name="cgls",
    )(block_ids.T, tile_counts, values, right_side)


def solution(mesh):
    both = ("slab", "sub")
    return jax.shard_map(
        functools.partial(per_device, mesh.shape["slab"], mesh.shape["sub"]),
        mesh=mesh,
        in_specs=(P(both, None, None, None), P(both, None), P("slab", "sub"), P(both, None)),
        out_specs=(P(both, None), P(both, None)),
        check_vma=False,
    )
```

time: 392 us -> 74 us (0.19)
  blocking collectives: 216 us -> 0 us
  starting transfers between devices: 73.9 us -> 0 us
  Pallas kernels: 0 us -> 69.9 us
  matrix products: 51.9 us -> 0 us
  waiting for transfers between devices: 23.5 us -> 0 us
  other arithmetic: 10.6 us -> 0 us
  between operations: 10.4 us -> 1.28 us
    psum x16 -> x0, blocking collectives: 169 us -> none  [one_axis_at_a_time(): return functools.reduce(lax.psum, axes, value)]
    pallas_call x0 -> x1, Pallas kernels: none -> 69.9 us  [per_device(): pl.pallas_call(functools.partial(kernel, slabs, subs, along_x), out_shape...]
    ppermute x18 -> x0, starting transfers between devices: 66.4 us -> none  [the longest x10 30.5 us: from_behind(): return lax.ppermute(block, axis, route)]
    dot_general x17 -> x0, matrix products: 51.9 us -> none  [the longest x4 29 us: forward(): image = jnp.einsum('tkij,tkj->ti', values, picked, precision=precise)]
    all_to_all x7 -> x0, blocking collectives: 47.9 us -> none  [the longest x4 27.4 us: copy_for_each(): return lax.all_to_all(copies, axis, split_axis=0, concat_axis=0, tiled=True)]
    ppermute x18 -> x0, waiting for transfers between devices: 14.6 us -> none  [the longest x10 10.4 us: from_behind(): return lax.ppermute(block, axis, route)]
    all_to_all x2 -> x0, waiting for transfers between devices: 8.85 us -> none  [sent_and_summed(): lax.all_to_all(parts, axis, split_axis=0, concat_axis=0, tiled=True)]
    all_to_all x2 -> x0, starting transfers between devices: 7.47 us -> none  [sent_and_summed(): lax.all_to_all(parts, axis, split_axis=0, concat_axis=0, tiled=True)]
  transfers between devices with their start and end apart: 20 -> 0, of which waited for: 9 -> 0; matrix products, arithmetic and copies ran while one was open for 1% -> 0% of each run, Pallas kernels for 0% -> 0%
where the time goes in v2:
time: 74 us; the launch traced here: 73.8 us
  Pallas kernels  69.9 us (94%)
  local copies, waits for them, and re-layouts  2.63 us (4%)
  between operations  1.28 us (2%)
    pallas_call x1, Pallas kernels, per_device(): pl.pallas_call(functools.partial(kernel, slabs, subs, along_x), out_shape...  69.9 us
    unnamed x2, local copies, waits for them, and re-layouts  2.63 us

profile of v2, /device:TPU:1, one launch (start us, length us, event | category | flops | bytes accessed | tf_op | source)
XLA Modules:
  0.0 73.8 jit_solution(9922344873956054049)
XLA Ops:
  1.3 69.9 %cgls.1 = (f32[12,256]{1,0:T(8,128)}, f32[24,128]{1,0:T(8,128)}) custom-call(s32[2,24]{1,0:T(2,128)} %bitcast.1, s32[1,1]{1,0:T(1,128)S(6)} %copy.8.count_ref, f32[24,2,128,256]{3,2,1,0:T(8,128)} %values_hbm.1, f32[24,128]{1,0:T(8,128)} %side_hbm.1), custom_call_target="tpu_custom_call" | custom-call | tf_op jit(solution)/shard_map/cgls/pallas_call | solution.py:509
  71.1 1.3 %copy.9 = f32[12,256]{1,0:T(8,128)} copy(f32[12,256]{1,0:T(8,128)} %get-tuple-element.4) | data formatting | bytes 24576
  72.5 1.3 %copy.10 = f32[24,128]{1,0:T(8,128)} copy(f32[24,128]{1,0:T(8,128)} %get-tuple-element.5) | data formatting | bytes 24576

commit v3 on v2

--- a/solution.py
+++ b/solution.py
@@ -39,23 +39,17 @@
     slabs,
     subs,
     along_x,
-    ids_hbm,
+    ids_ref,
     count_ref,
     values_hbm,
-    side_hbm,
+    side,
     solution_ref,
     residual_ref,
     values,
-    side,
-    ids_ref,
     columns,
     ids_buf,
-    first_terms,
     terms,
-    first_sums,
     sums,
-    first_near,
-    first_far,
     near,
     far,
     window,
@@ -63,8 +57,6 @@
     plane,
     depth,
     load_sem,
-    side_sem,
-    index_sem,
     ids_send,
     ids_recv,
     term_send,
@@ -108,10 +100,6 @@
         return pl.ds(128 * half, 128)
 
     group = tiles // GROUPS
-    side_load = pltpu.make_async_copy(side_hbm, side, side_sem)
-    side_load.start()
-    ids_load = pltpu.make_async_copy(ids_hbm, ids_ref, index_sem)
-    ids_load.start()
     loads = []
     for half in range(2):
         for part in range(GROUPS):
@@ -135,7 +123,6 @@
 
     base = (slab - 1) * nodes
     count = count_ref[0, 0]
-    ids_load.wait()
     lanes = lax.broadcasted_iota(jnp.int32, (1, 256), 1)
     ids_row = jnp.zeros((1, 256), jnp.int32)
     for tile in range(tiles):
@@ -145,7 +132,6 @@
     ids_buf[sub] = ids_row
 
     live_rows = lax.broadcasted_iota(jnp.int32, (tiles, 128), 0) < count
-    side_load.wait()
     residual = jnp.where(live_rows, side[...], 0.0)
     rows[...] = residual
     eye = lax.broadcasted_iota(jnp.int32, (128, 128), 0) == lax.broadcasted_iota(
@@ -185,8 +171,8 @@
         for slot in range(2):
             block = values[tile, slot, :, 128 * half : 128 * (half + 1)]
             at = place_of(tile, slot)
-            first_terms[half, 0, at, :] = jnp.sum(block * column, axis=0, keepdims=True)
-            first_terms[half, 1, at, :] = jnp.sum(block * block, axis=0, keepdims=True) * live
+            terms[0, half, at, :] = jnp.sum(block * column, axis=0, keepdims=True)
+            terms[1, half, at, :] = jnp.sum(block * block, axis=0, keepdims=True) * live
 
     def image_of(tile):
         live = live_of(tile)
@@ -209,21 +195,21 @@
             column = columns[tile]
         for slot in range(2):
             block = values[tile, slot, :, 128 * half : 128 * (half + 1)]
-            terms[phase, half, 0, place_of(tile, slot), :] = jnp.sum(
+            terms[phase, half, place_of(tile, slot), :] = jnp.sum(
                 block * column, axis=0, keepdims=True
             )
 
-    def spread(terms_ref, phase, half):
-        part = terms_ref.at[half, :, pl.ds(sub * own, own)]
+    def spread(phase, half, part):
+        at = terms.at[phase, half, pl.ds(sub * own + 2 * part * group, 2 * group)]
         return [
             copy(
-                part,
-                part,
-                term_send.at[phase, half, step],
-                term_recv.at[phase, half, step],
+                at,
+                at,
+                term_send.at[phase, half, part, step],
+                term_recv.at[phase, half, part, step],
                 sub_peer(step),
             )
-            for step in range(1, subs)
+            for step in sorted(range(1, subs), key=lambda step: -min(step, subs - step))
         ]
 
     def arrived(items):
@@ -239,20 +225,18 @@
             jnp.dot(selector, piece, preferred_element_type=F32) for piece in (high, middle, low)
         )
 
-    def exchange(terms_ref, sums_ref, near_ref, far_ref, phase, half):
-        mine = []
-        for index in range(terms_ref.shape[1]):
-            mine.append(summed(terms_ref[half, index]))
-            sums_ref[half, index] = mine[index]
+    def exchange(phase, half):
+        mine = summed(terms[phase, half])
+        sums[phase, half] = mine
         moves = (
-            (1, pl.ds(nodes, 2 * nodes), near_ref.at[half, 0]),
-            (-1, pl.ds(0, 2 * nodes), near_ref.at[half, 1]),
-            (2, pl.ds(2 * nodes, nodes), far_ref.at[half, 0]),
-            (-2, pl.ds(0, nodes), far_ref.at[half, 1]),
+            (2, pl.ds(2 * nodes, nodes), far.at[phase, half, 0]),
+            (-2, pl.ds(0, nodes), far.at[phase, half, 1]),
+            (1, pl.ds(nodes, 2 * nodes), near.at[phase, half, 0]),
+            (-1, pl.ds(0, 2 * nodes), near.at[phase, half, 1]),
         )
         items = [
             copy(
-                sums_ref.at[half, :, part],
+                sums.at[phase, half, part],
                 target,
                 sum_send.at[phase, half, place],
                 sum_recv.at[phase, half, place],
@@ -262,21 +246,18 @@
         ]
         return mine, items
 
-    def combined(mine, near_ref, far_ref, half):
-        found = []
-        for index, value in enumerate(mine):
-            below, above = near_ref[half, 0, index], near_ref[half, 1, index]
-            found.append(
-                jnp.concatenate(
-                    [
-                        (far_ref[half, 0, index] + below[:nodes]) + value[:nodes],
-                        (below[nodes:] + value[nodes : 2 * nodes]) + above[:nodes],
-                        (value[2 * nodes :] + above[nodes:]) + far_ref[half, 1, index],
-                    ],
-                    axis=0,
-                )
-            )
-        return found
+    def result(phase, half, moved):
+        value, items = moved
+        arrived(items)
+        below, above = near[phase, half, 0], near[phase, half, 1]
+        return jnp.concatenate(
+            [
+                (far[phase, half, 0] + below[:nodes]) + value[:nodes],
+                (below[nodes:] + value[nodes : 2 * nodes]) + above[:nodes],
+                (value[2 * nodes :] + above[nodes:]) + far[phase, half, 1],
+            ],
+            axis=0,
+        )
 
     def start_plane(index, row):
         plane[index, plane_at] = row
@@ -305,116 +286,104 @@
     def dot(one, other):
         return total(one[0] * other[0] + one[1] * other[1]) * (1.0 / subs)
 
-    items = []
+    items = {(phase, half): [] for phase in range(2) for half in range(2)}
     for half in range(2):
         for part in range(GROUPS):
             loads[half * GROUPS + part].wait()
 
-            @pl.loop(part * group, (part + 1) * group, unroll=2)
+            @pl.loop(part * group, (part + 1) * group, unroll=4)
             def _(tile):
                 first_tile(tile, half)
 
-        if half == 0:
-            pl.semaphore_wait(barrier, len(partners))
-            place = ids_buf.at[sub]
-            ids_items = [
-                copy(place, place, ids_send.at[step], ids_recv.at[step], sub_peer(step))
-                for step in range(1, subs)
-            ]
-        items.append(spread(first_terms, 0, half))
+            if half == 0 and part == 0:
+                pl.semaphore_wait(barrier, len(partners))
+                place = ids_buf.at[sub]
+                ids_items = [
+                    copy(place, place, ids_send.at[step], ids_recv.at[step], sub_peer(step))
+                    for step in range(1, subs)
+                ]
+            for phase in range(2):
+                items[phase, half] += spread(phase, half, part)
     arrived(ids_items)
     all_ids = sum(ids_buf[i] for i in range(subs))[:, : subs * own]
     row_ids = lax.broadcasted_iota(jnp.int32, (3 * nodes, subs * own), 0) + 1
     selector = jnp.where(row_ids == all_ids, 1.0, 0.0).astype(BF16)
-    moved = []
-    for half in range(2):
-        arrived(items[half])
-        moved.append(exchange(first_terms, first_sums, first_near, first_far, 0, half))
+    moved = {}
+    for half in range(2):
+        for phase in range(2):
+            arrived(items[phase, half])
+            moved[phase, half] = exchange(phase, half)
     normal, jacobi, u_all = [], [], []
     for half in range(2):
-        mine, items = moved[half]
-        arrived(items)
-        found, squares = combined(mine, first_near, first_far, half)
-        normal.append(found)
-        jacobi.append(1.0 / (1.0 + squares))
-        u_all.append(jacobi[half] * found)
+        normal.append(result(0, half, moved[0, half]))
+        jacobi.append(1.0 / (1.0 + result(1, half, moved[1, half])))
+        u_all.append(jacobi[half] * normal[half])
         window[half] = u_all[half]
 
-    def applied(phase, dots):
-        items = []
+    def applied(phase, meanwhile):
+        items = [[], []]
         for half in range(2):
-
-            @pl.loop(0, tiles, unroll=4)
-            def _(tile):
-                back_tile(phase, tile, half)
-
-            items.append(spread(terms.at[phase], 1 + phase, half))
-        later = dots() if dots is not None else None
+            for part in range(GROUPS):
+
+                @pl.loop(part * group, (part + 1) * group, unroll=4)
+                def _(tile):
+                    back_tile(phase, tile, half)
+
+                items[half] += spread(phase, half, part)
+        found = meanwhile()
         moved = []
         for half in range(2):
             arrived(items[half])
-            moved.append(
-                exchange(
-                    terms.at[phase],
-                    sums.at[phase],
-                    near.at[phase],
-                    far.at[phase],
-                    1 + phase,
-                    half,
-                )
-            )
-        return moved, later
-
-    def result(phase, moved, half):
-        mine, items = moved[half]
-        arrived(items)
-        return combined(mine, near.at[phase], far.at[phase], half)[0]
+            moved.append(exchange(phase, half))
+        return moved, found
 
     r, u = middle_of(normal), middle_of(u_all)
 
-    def dots_0():
+    def beside_0():
         a_row = rows[...]
-        return start_plane(0, packed([dot(r, u), total(a_row * a_row)]))
-
-    moved, reducing = applied(0, dots_0)
-    a_row = rows[...]
+        return start_plane(0, packed([dot(r, u), total(a_row * a_row)])), a_row
+
+    moved, (reducing, a_row) = applied(2, beside_0)
     w_all, m_all = [], []
     for half in range(2):
-        w_all.append(result(0, moved, half))
+        w_all.append(result(2, half, moved[half]))
         m_all.append(jacobi[half] * w_all[half])
         window[half] = m_all[half]
+
     w, m = middle_of(w_all), middle_of(m_all)
 
-    def dots_1():
+    def beside_1():
         g_row = rows[...]
-        return start_plane(
+        later = start_plane(
             1, packed([dot(w, u), dot(w, m), total(a_row * g_row), total(g_row * g_row)])
         )
-
-    reducing = start_depth(0, reducing)
-    moved, later = applied(1, dots_1)
-    g_row = rows[...]
+        return start_depth(0, reducing), later, g_row
+
+    moved, (reducing, later, g_row) = applied(3, beside_1)
     rho, norm = finish_depth(0, reducing, 2)
     reducing = start_depth(1, later)
     alpha = rho / norm
     z_all = []
     for half in range(2):
-        z_all.append(result(1, moved, half))
+        z_all.append(result(3, half, moved[half]))
         w_all[half] = w_all[half] - alpha * z_all[half]
         window[half] = jacobi[half] * w_all[half]
-        m_all[half] = jacobi[half] * w_all[half]
-    q, s, p = m, w, u
+    old_rho, old_norm, old_alpha = rho, norm, alpha
+
+    def beside_2():
+        q, s, p = m, w, u
+        x = [old_alpha * one for one in p]
+        new_u = [one - old_alpha * other for one, other in zip(u, q)]
+        new_r = [one - old_alpha * other for one, other in zip(r, s)]
+        new_residual = residual - old_alpha * a_row
+        new_a = a_row - old_alpha * g_row
+        new_w = middle_of(w_all)
+        new_m = [jacobi[half][nodes : 2 * nodes] * new_w[half] for half in range(2)]
+        return q, s, p, x, new_u, new_r, new_residual, new_a, new_w, new_m, rows[...]
+
+    moved, kept = applied(4, beside_2)
     ap_row, aq_row = a_row, g_row
-    x = [alpha * one for one in p]
-    u = [one - alpha * other for one, other in zip(u, q)]
-    r = [one - alpha * other for one, other in zip(r, s)]
-    residual = residual - alpha * ap_row
-    a_row = a_row - alpha * aq_row
-    w, m = middle_of(w_all), middle_of(m_all)
-    old_rho, old_norm, old_alpha = rho, norm, alpha
-
-    moved, _ = applied(2, None)
-    g_row = rows[...]
+    q, s, p, x, u, r, residual, a_row, w, m, g_row = kept
     w_u, w_m, a_g, g_g = finish_depth(1, reducing, 4)
     rho = old_rho - 2.0 * old_alpha * w_u + old_alpha * old_alpha * w_m
     beta = rho / old_rho
@@ -425,10 +394,6 @@
         + old_alpha * old_alpha * g_g
     )
     alpha = rho / norm
-    for half in range(2):
-        z_all[half] = result(2, moved, half) + beta * z_all[half]
-        w_all[half] = w_all[half] - alpha * z_all[half]
-        window[half] = jacobi[half] * w_all[half]
     q = [one + beta * other for one, other in zip(m, q)]
     s = [one + beta * other for one, other in zip(w, s)]
     p = [one + beta * other for one, other in zip(u, p)]
@@ -439,6 +404,10 @@
     aq_row = g_row + beta * aq_row
     residual = residual - alpha * ap_row
     a_row = a_row - alpha * aq_row
+    for half in range(2):
+        z_all[half] = result(4, half, moved[half]) + beta * z_all[half]
+        w_all[half] = w_all[half] - alpha * z_all[half]
+        window[half] = jacobi[half] * w_all[half]
     w = middle_of(w_all)
     m = [window[half, pl.ds(nodes, nodes)] for half in range(2)]
     rho_1, norm_1 = rho, norm
@@ -513,10 +482,10 @@
             jax.ShapeDtypeStruct((tiles, height), F32),
         ),
         in_specs=[
-            pl.BlockSpec(memory_space=pl.ANY),
+            pl.BlockSpec(memory_space=pltpu.SMEM),
             pl.BlockSpec(memory_space=pltpu.SMEM),
             pl.BlockSpec(memory_space=pl.ANY),
-            pl.BlockSpec(memory_space=pl.ANY),
+            pl.BlockSpec(memory_space=pltpu.VMEM),
         ],
         out_specs=(
             pl.BlockSpec(memory_space=pltpu.VMEM),
@@ -524,38 +493,30 @@
         ),
         scratch_shapes=[
             vmem(values.shape, F32),
-            vmem((tiles, height), F32),
-            pltpu.SMEM((2, tiles), jnp.int32),
             vmem((tiles, height, half), F32),
             vmem((subs, 1, 256), jnp.int32),
-            vmem((2, 2, subs * own, half), F32),
-            vmem((3, 2, 1, subs * own, half), F32),
-            vmem((2, 2, 3 * nodes, half), F32),
-            vmem((3, 2, 1, 3 * nodes, half), F32),
-            vmem((2, 2, 2, 2 * nodes, half), F32),
-            vmem((2, 2, 2, nodes, half), F32),
-            vmem((3, 2, 2, 1, 2 * nodes, half), F32),
-            vmem((3, 2, 2, 1, nodes, half), F32),
+            vmem((5, 2, subs * own, half), F32),
+            vmem((5, 2, 3 * nodes, half), F32),
+            vmem((5, 2, 2, 2 * nodes, half), F32),
+            vmem((5, 2, 2, nodes, half), F32),
             vmem((2, 3 * nodes, half), F32),
             vmem((tiles, height), F32),
             vmem((3, plane_count, 1, 128), F32),
             vmem((3, depth_count, 1, 128), F32),
             dma((2 * GROUPS,)),
-            dma,
-            dma,
             dma((subs,)),
             dma((subs,)),
-            dma((4, 2, subs)),
-            dma((4, 2, subs)),
-            dma((4, 2, 4)),
-            dma((4, 2, 4)),
+            dma((5, 2, GROUPS, subs)),
+            dma((5, 2, GROUPS, subs)),
+            dma((5, 2, 4)),
+            dma((5, 2, 4)),
             dma((3, plane_count)),
             dma((3, plane_count)),
             dma((3, depth_count)),
             dma((3, depth_count)),
         ],
         compiler_params=pltpu.CompilerParams(
-            collective_id=0, has_side_effects=True, vmem_limit_bytes=67043328
+            collective_id=0, has_side_effects=True, vmem_limit_bytes=48 * 1024 * 1024
         ),
         name="cgls",
     )(block_ids.T, tile_counts, values, right_side)

time: 74 us -> 73 us (0.986)
  Pallas kernels: 69.9 us -> 68.9 us
    pallas_call x1, Pallas kernels: 69.9 us -> 68.9 us  [per_device(): pl.pallas_call(functools.partial(kernel, slabs, subs, along_x), out_shape...]
    unnamed x2 -> x6, local copies, waits for them, and re-layouts: 2.63 us -> 2.59 us
where the time goes in v3:
time: 73 us; the launch traced here: 72.8 us
  Pallas kernels  68.9 us (94%)
  local copies, waits for them, and re-layouts  2.59 us (4%)
  between operations  1.29 us (2%)
    pallas_call x1, Pallas kernels, per_device(): pl.pallas_call(functools.partial(kernel, slabs, subs, along_x), out_shape...  68.9 us
    unnamed x6, local copies, waits for them, and re-layouts  2.59 us

profile of v3, /device:TPU:1, one launch (start us, length us, event | category | flops | bytes accessed | tf_op | source)
XLA Modules:
  0.0 72.8 jit_solution(12970467524608710938)
XLA Ops:
  1.3 0.0 copy-start
  1.3 0.7 copy-done
  2.0 0.0 copy-start.1
  2.0 0.7 copy-done.1
  2.7 68.9 %cgls.1 = (f32[12,256]{1,0:T(8,128)S(1)}, f32[24,128]{1,0:T(8,128)S(1)}) custom-call(s32[2,24]{1,0:T(2,128)S(1)} %bitcast.1, s32[1,1]{1,0:T(1,128)S(6)} %copy.8.count_ref, f32[24,2,128,256]{3,2,1,0:T(8,128)} %values_hbm.1, f32[24,128]{1,0:T(8,128)S(1)} %copy-done), custom_call_target="tpu_custom_call" | custom-call | tf_op jit(solution)/shard_map/cgls/pallas_call | solution.py:478
  71.6 0.6 copy.9
  72.2 0.6 copy.10
Async XLA Ops:
  1.3 0.7 copy-start
  2.0 0.7 copy-start.1

commit v4 on v3

--- a/solution.py
+++ b/solution.py
@@ -11,7 +11,8 @@
 NODES = 12
 CORES = 2
 ALONG_X = 4
-GROUPS = 3
+GROUPS = 1
+LOADS = 3
 F32 = jnp.float32
 BF16 = jnp.bfloat16
 
@@ -100,13 +101,14 @@
         return pl.ds(128 * half, 128)
 
     group = tiles // GROUPS
+    share = tiles // LOADS
     loads = []
     for half in range(2):
-        for part in range(GROUPS):
-            at = (pl.ds(part * group, group), slice(None), slice(None), half_of(half))
+        for part in range(LOADS):
+            at = (pl.ds(part * share, share), slice(None), slice(None), half_of(half))
             loads.append(
                 pltpu.make_async_copy(
-                    values_hbm.at[at], values.at[at], load_sem.at[half * GROUPS + part]
+                    values_hbm.at[at], values.at[at], load_sem.at[half * LOADS + part]
                 )
             )
     for load in loads:
@@ -174,16 +176,23 @@
             terms[0, half, at, :] = jnp.sum(block * column, axis=0, keepdims=True)
             terms[1, half, at, :] = jnp.sum(block * block, axis=0, keepdims=True) * live
 
-    def image_of(tile):
+    def picked(tile, half):
         live = live_of(tile)
         product = None
         for slot in range(2):
             at = jnp.minimum(jnp.maximum(ids_ref[slot, tile] - base, 0), 3 * nodes - 1)
-            for half in range(2):
-                row = window[half, pl.ds(at, 1), :] * live
-                part = values[tile, slot, :, 128 * half : 128 * (half + 1)] * row
-                product = part if product is None else product + part
-        column = jnp.sum(product, axis=1, keepdims=True)
+            row = window[half, pl.ds(at, 1), :] * live
+            part = values[tile, slot, :, 128 * half : 128 * (half + 1)] * row
+            product = part if product is None else product + part
+        return product
+
+    def begin_images():
+        @pl.loop(0, tiles, unroll=8)
+        def _(tile):
+            columns[tile] = picked(tile, 0)
+
+    def image_of(tile):
+        column = jnp.sum(columns[tile] + picked(tile, 1), axis=1, keepdims=True)
         rows[pl.ds(tile, 1), :] = jnp.sum(jnp.where(eye, column, 0.0), axis=0, keepdims=True)
         return column
 
@@ -288,22 +297,22 @@
 
     items = {(phase, half): [] for phase in range(2) for half in range(2)}
     for half in range(2):
-        for part in range(GROUPS):
-            loads[half * GROUPS + part].wait()
-
-            @pl.loop(part * group, (part + 1) * group, unroll=4)
+        for part in range(LOADS):
+            loads[half * LOADS + part].wait()
+
+            @pl.loop(part * share, (part + 1) * share, unroll=4)
             def _(tile):
                 first_tile(tile, half)
 
-            if half == 0 and part == 0:
-                pl.semaphore_wait(barrier, len(partners))
-                place = ids_buf.at[sub]
-                ids_items = [
-                    copy(place, place, ids_send.at[step], ids_recv.at[step], sub_peer(step))
-                    for step in range(1, subs)
-                ]
-            for phase in range(2):
-                items[phase, half] += spread(phase, half, part)
+        if half == 0:
+            pl.semaphore_wait(barrier, len(partners))
+            place = ids_buf.at[sub]
+            ids_items = [
+                copy(place, place, ids_send.at[step], ids_recv.at[step], sub_peer(step))
+                for step in range(1, subs)
+            ]
+        for phase in range(2):
+            items[phase, half] += spread(phase, half, 0)
     arrived(ids_items)
     all_ids = sum(ids_buf[i] for i in range(subs))[:, : subs * own]
     row_ids = lax.broadcasted_iota(jnp.int32, (3 * nodes, subs * own), 0) + 1
@@ -319,13 +328,15 @@
         jacobi.append(1.0 / (1.0 + result(1, half, moved[1, half])))
         u_all.append(jacobi[half] * normal[half])
         window[half] = u_all[half]
+        if half == 0:
+            begin_images()
 
     def applied(phase, meanwhile):
         items = [[], []]
         for half in range(2):
             for part in range(GROUPS):
 
-                @pl.loop(part * group, (part + 1) * group, unroll=4)
+                @pl.loop(part * group, (part + 1) * group, unroll=12)
                 def _(tile):
                     back_tile(phase, tile, half)
 
@@ -349,6 +360,8 @@
         w_all.append(result(2, half, moved[half]))
         m_all.append(jacobi[half] * w_all[half])
         window[half] = m_all[half]
+        if half == 0:
+            begin_images()
 
     w, m = middle_of(w_all), middle_of(m_all)
 
@@ -368,6 +381,8 @@
         z_all.append(result(3, half, moved[half]))
         w_all[half] = w_all[half] - alpha * z_all[half]
         window[half] = jacobi[half] * w_all[half]
+        if half == 0:
+            begin_images()
     old_rho, old_norm, old_alpha = rho, norm, alpha
 
     def beside_2():
@@ -408,6 +423,8 @@
         z_all[half] = result(4, half, moved[half]) + beta * z_all[half]
         w_all[half] = w_all[half] - alpha * z_all[half]
         window[half] = jacobi[half] * w_all[half]
+        if half == 0:
+            begin_images()
     w = middle_of(w_all)
     m = [window[half, pl.ds(nodes, nodes)] for half in range(2)]
     rho_1, norm_1 = rho, norm
@@ -503,7 +520,7 @@
             vmem((tiles, height), F32),
             vmem((3, plane_count, 1, 128), F32),
             vmem((3, depth_count, 1, 128), F32),
-            dma((2 * GROUPS,)),
+            dma((2 * LOADS,)),
             dma((subs,)),
             dma((subs,)),
             dma((5, 2, GROUPS, subs)),

time: 73 us -> 70.8 us (0.970)
  Pallas kernels: 68.9 us -> 66.7 us
    pallas_call x1, Pallas kernels: 68.9 us -> 66.7 us  [per_device(): pl.pallas_call(functools.partial(kernel, slabs, subs, along_x), out_shape...]
where the time goes in v4:
time: 70.8 us; the launch traced here: 70.6 us
  Pallas kernels  66.7 us (94%)
  local copies, waits for them, and re-layouts  2.59 us (4%)
  between operations  1.29 us (2%)
    pallas_call x1, Pallas kernels, per_device(): pl.pallas_call(functools.partial(kernel, slabs, subs, along_x), out_shape...  66.7 us
    unnamed x6, local copies, waits for them, and re-layouts  2.59 us

profile of v4, /device:TPU:1, one launch (start us, length us, event | category | flops | bytes accessed | tf_op | source)
XLA Modules:
  0.0 70.6 jit_solution(15385366799779510478)
XLA Ops:
  1.3 0.0 copy-start
  1.3 0.7 copy-done
  2.0 0.0 copy-start.1
  2.0 0.7 copy-done.1
  2.7 66.7 %cgls.1 = (f32[12,256]{1,0:T(8,128)S(1)}, f32[24,128]{1,0:T(8,128)S(1)}) custom-call(s32[2,24]{1,0:T(2,128)S(1)} %bitcast.1, s32[1,1]{1,0:T(1,128)S(6)} %copy.8.count_ref, f32[24,2,128,256]{3,2,1,0:T(8,128)} %values_hbm.1, f32[24,128]{1,0:T(8,128)S(1)} %copy-done), custom_call_target="tpu_custom_call" | custom-call | tf_op jit(solution)/shard_map/cgls/pallas_call | solution.py:495
  69.4 0.6 copy.9
  70.0 0.6 copy.10
Async XLA Ops:
  1.3 0.7 %copy-start = (f32[24,128]{1,0:T(8,128)S(1)}, f32[24,128]{1,0:T(8,128)}, u32[]{:S(2)}) copy-start(f32[24,128]{1,0:T(8,128)} %side.1) | copy-start | bytes 36868
  2.0 0.7 copy-start.1

commit v5 on v4

--- a/solution.py
+++ b/solution.py
@@ -187,7 +187,7 @@
         return product
 
     def begin_images():
-        @pl.loop(0, tiles, unroll=8)
+        @pl.loop(0, tiles, unroll=12)
         def _(tile):
             columns[tile] = picked(tile, 0)
 
@@ -439,7 +439,7 @@
         dot(s, q),
     ]
 
-    @pl.loop(0, tiles, unroll=4)
+    @pl.loop(0, tiles, unroll=24)
     def _(tile):
         image_of(tile)
 
@@ -447,7 +447,13 @@
     fields = [a_row, g_row, aq_row, ap_row]
     pairs = [(i, j) for i in range(4) for j in range(i, 4)]
     row_dots = [total(fields[i] * fields[j]) for i, j in pairs]
-    later = start_depth(2, start_plane(2, packed(node_dots + row_dots)))
+    before = len(sent)
+    planes = start_plane(2, packed(node_dots + row_dots))
+    for item in sent[:before]:
+        item.wait_send()
+    later = start_depth(2, planes)
+    for item in planes:
+        item.wait_send()
     found = finish_depth(2, later, len(node_dots) + len(pairs))
     rho_2, uu, cross, s_u, w_m, s_m, s_q = found[: len(node_dots)]
     gram = dict(zip(pairs, found[len(node_dots) :]))
@@ -478,7 +484,7 @@
         for index in range(1, subs):
             mine = jnp.where(sub == index, x[half][index * NODES : (index + 1) * NODES], mine)
         solution_ref[:, 128 * half : 128 * (half + 1)] = mine
-    for item in sent:
+    for item in later:
         item.wait_send()
 
 

time: 70.8 us -> 69.9 us (0.987)
  Pallas kernels: 66.7 us -> 65.9 us
    pallas_call x1, Pallas kernels: 66.7 us -> 65.9 us  [per_device(): pl.pallas_call(functools.partial(kernel, slabs, subs, along_x), out_shape...]
where the time goes in v5:
time: 69.9 us; the launch traced here: 69.7 us
  Pallas kernels  65.9 us (94%)
  local copies, waits for them, and re-layouts  2.59 us (4%)
  between operations  1.29 us (2%)
    pallas_call x1, Pallas kernels, per_device(): pl.pallas_call(functools.partial(kernel, slabs, subs, along_x), out_shape...  65.9 us
    unnamed x6, local copies, waits for them, and re-layouts  2.59 us

profile of v5, /device:TPU:1, one launch (start us, length us, event | category | flops | bytes accessed | tf_op | source)
XLA Modules:
  0.0 69.7 jit_solution(15986898092229591915)
XLA Ops:
  1.3 0.0 copy-start
  1.3 0.7 %copy-done = f32[24,128]{1,0:T(8,128)S(1)} copy-done((f32[24,128]{1,0:T(8,128)S(1)}, f32[24,128]{1,0:T(8,128)}, u32[]{:S(2)}) %copy-start) | copy-done | bytes 12312
  2.0 0.0 copy-start.1
  2.0 0.7 copy-done.1
  2.7 65.9 %cgls.1 = (f32[12,256]{1,0:T(8,128)S(1)}, f32[24,128]{1,0:T(8,128)S(1)}) custom-call(s32[2,24]{1,0:T(2,128)S(1)} %bitcast.1, s32[1,1]{1,0:T(1,128)S(6)} %copy.8.count_ref, f32[24,2,128,256]{3,2,1,0:T(8,128)} %values_hbm.1, f32[24,128]{1,0:T(8,128)S(1)} %copy-done), custom_call_target="tpu_custom_call" | custom-call | tf_op jit(solution)/shard_map/cgls/pallas_call | solution.py:501
  68.5 0.6 copy.9
  69.1 0.6 copy.10
Async XLA Ops:
  1.3 0.7 %copy-start = (f32[24,128]{1,0:T(8,128)S(1)}, f32[24,128]{1,0:T(8,128)}, u32[]{:S(2)}) copy-start(f32[24,128]{1,0:T(8,128)} %side.1) | copy-start | bytes 36868
  2.0 0.7 copy-start.1

commit v6 on v5

--- a/solution.py
+++ b/solution.py
@@ -192,9 +192,10 @@
             columns[tile] = picked(tile, 0)
 
     def image_of(tile):
-        column = jnp.sum(columns[tile] + picked(tile, 1), axis=1, keepdims=True)
+        return jnp.sum(columns[tile] + picked(tile, 1), axis=1, keepdims=True)
+
+    def keep_row(tile, column):
         rows[pl.ds(tile, 1), :] = jnp.sum(jnp.where(eye, column, 0.0), axis=0, keepdims=True)
-        return column
 
     def back_tile(phase, tile, half):
         if half == 0:
@@ -341,6 +342,11 @@
                     back_tile(phase, tile, half)
 
                 items[half] += spread(phase, half, part)
+
+        @pl.loop(0, tiles, unroll=12)
+        def _(tile):
+            keep_row(tile, columns[tile])
+
         found = meanwhile()
         moved = []
         for half in range(2):
@@ -441,7 +447,7 @@
 
     @pl.loop(0, tiles, unroll=24)
     def _(tile):
-        image_of(tile)
+        keep_row(tile, image_of(tile))
 
     g_row = rows[...]
     fields = [a_row, g_row, aq_row, ap_row]

time: 69.9 us -> 69.7 us (level)
  no operation moved by 1% of the time
where the time goes in v6:
time: 69.7 us; the launch traced here: 69.6 us
  Pallas kernels  65.7 us (94%)
  local copies, waits for them, and re-layouts  2.59 us (4%)
  between operations  1.29 us (2%)
    pallas_call x1, Pallas kernels, per_device(): pl.pallas_call(functools.partial(kernel, slabs, subs, along_x), out_shape...  65.7 us
    unnamed x6, local copies, waits for them, and re-layouts  2.59 us

profile of v6, /device:TPU:1, one launch (start us, length us, event | category | flops | bytes accessed | tf_op | source)
XLA Modules:
  0.0 69.6 jit_solution(5832823438346590679)
XLA Ops:
  1.3 0.0 copy-start
  1.3 0.7 %copy-done = f32[24,128]{1,0:T(8,128)S(1)} copy-done((f32[24,128]{1,0:T(8,128)S(1)}, f32[24,128]{1,0:T(8,128)}, u32[]{:S(2)}) %copy-start) | copy-done | bytes 12312
  2.0 0.0 copy-start.1
  2.0 0.7 copy-done.1
  2.7 65.7 %cgls.1 = (f32[12,256]{1,0:T(8,128)S(1)}, f32[24,128]{1,0:T(8,128)S(1)}) custom-call(s32[2,24]{1,0:T(2,128)S(1)} %bitcast.1, s32[1,1]{1,0:T(1,128)S(6)} %copy.8.count_ref, f32[24,2,128,256]{3,2,1,0:T(8,128)} %values_hbm.1, f32[24,128]{1,0:T(8,128)S(1)} %copy-done), custom_call_target="tpu_custom_call" | custom-call | tf_op jit(solution)/shard_map/cgls/pallas_call | solution.py:507
  68.4 0.6 copy.9
  69.0 0.6 copy.10
Async XLA Ops:
  1.3 0.7 %copy-start = (f32[24,128]{1,0:T(8,128)S(1)}, f32[24,128]{1,0:T(8,128)}, u32[]{:S(2)}) copy-start(f32[24,128]{1,0:T(8,128)} %side.1) | copy-start | bytes 36868
  2.0 0.7 copy-start.1

commit v7 on v6

--- a/solution.py
+++ b/solution.py
@@ -301,7 +301,7 @@
         for part in range(LOADS):
             loads[half * LOADS + part].wait()
 
-            @pl.loop(part * share, (part + 1) * share, unroll=4)
+            @pl.loop(part * share, (part + 1) * share, unroll=8)
             def _(tile):
                 first_tile(tile, half)
 
@@ -337,7 +337,7 @@
         for half in range(2):
             for part in range(GROUPS):
 
-                @pl.loop(part * group, (part + 1) * group, unroll=12)
+                @pl.loop(part * group, (part + 1) * group, unroll=24)
                 def _(tile):
                     back_tile(phase, tile, half)
 

time: 69.7 us -> 69.5 us (level)
  no operation moved by 1% of the time
where the time goes in v7:
time: 69.5 us; the launch traced here: 69.4 us
  Pallas kernels  65.5 us (94%)
  local copies, waits for them, and re-layouts  2.59 us (4%)
  between operations  1.29 us (2%)
    pallas_call x1, Pallas kernels, per_device(): pl.pallas_call(functools.partial(kernel, slabs, subs, along_x), out_shape...  65.5 us
    unnamed x6, local copies, waits for them, and re-layouts  2.59 us

profile of v7, /device:TPU:1, one launch (start us, length us, event | category | flops | bytes accessed | tf_op | source)
XLA Modules:
  0.0 69.4 jit_solution(6091182702680902881)
XLA Ops:
  1.3 0.0 copy-start
  1.3 0.7 %copy-done = f32[24,128]{1,0:T(8,128)S(1)} copy-done((f32[24,128]{1,0:T(8,128)S(1)}, f32[24,128]{1,0:T(8,128)}, u32[]{:S(2)}) %copy-start) | copy-done | bytes 12312
  2.0 0.0 copy-start.1
  2.0 0.7 copy-done.1
  2.7 65.5 %cgls.1 = (f32[12,256]{1,0:T(8,128)S(1)}, f32[24,128]{1,0:T(8,128)S(1)}) custom-call(s32[2,24]{1,0:T(2,128)S(1)} %bitcast.1, s32[1,1]{1,0:T(1,128)S(6)} %copy.8.count_ref, f32[24,2,128,256]{3,2,1,0:T(8,128)} %values_hbm.1, f32[24,128]{1,0:T(8,128)S(1)} %copy-done), custom_call_target="tpu_custom_call" | custom-call | tf_op jit(solution)/shard_map/cgls/pallas_call | solution.py:507
  68.1 0.6 copy.9
  68.8 0.6 copy.10
Async XLA Ops:
  1.3 0.7 %copy-start = (f32[24,128]{1,0:T(8,128)S(1)}, f32[24,128]{1,0:T(8,128)}, u32[]{:S(2)}) copy-start(f32[24,128]{1,0:T(8,128)} %side.1) | copy-start | bytes 36868
  2.0 0.7 copy-start.1
